TPU v7x, 8 devices: a whole 2x2x1 slice. The times are simulated.
8 devices in a mesh: dp: 1 (over z), col: 2 (over y), row: 4 (over x, core).
Axes of the slice: x: 2, y: 2, z: 1, core: 2. Of those that a mesh axis runs over, the one named last changes fastest.
Arguments:
- h_first: bfloat16 [128, 768], P(('dp', 'col', 'row'))
- h_second: bfloat16 [128, 768], P(('dp', 'col', 'row'))
- start_pos: int32 [128], P(('dp', 'col', 'row'))
- enc_lens: int32 [128], P(('dp', 'col', 'row'))
- dec_bias: float32 [32, 12], replicated
- norm_self: bfloat16 [2, 768], replicated
- norm_cross: bfloat16 [2, 768], replicated
- norm_mlp: bfloat16 [2, 768], replicated
- w_query: bfloat16 [2, 768, 768], P(None, 'row', 'col')
- w_key: bfloat16 [2, 768, 768], P(None, 'row', 'col')
- w_value: bfloat16 [2, 768, 768], P(None, 'row', 'col')
- w_out: bfloat16 [2, 768, 768], P(None, 'row', 'col')
- w_cquery: bfloat16 [2, 768, 768], P(None, 'row', 'col')
- w_cout: bfloat16 [2, 768, 768], P(None, 'row', 'col')
- w_gate: bfloat16 [2, 768, 2048], P(None, 'row', 'col')
- w_up: bfloat16 [2, 768, 2048], P(None, 'row', 'col')
- w_down: bfloat16 [2, 2048, 768], P(None, 'row', 'col')
- self_k: bfloat16 [2, 128, 512, 12, 64], P(None, ('dp', 'col', 'row'))
- self_v: bfloat16 [2, 128, 512, 12, 64], P(None, ('dp', 'col', 'row'))
- cross_k: bfloat16 [2, 128, 512, 12, 64], P(None, ('dp', 'col', 'row'))
- cross_v: bfloat16 [2, 128, 512, 12, 64], P(None, ('dp', 'col', 'row'))
Outputs:
- output 1: bfloat16 [2, 128, 768], P(None, ('dp', 'col', 'row'))
- output 2: bfloat16 [2, 128, 512, 12, 64], P(None, ('dp', 'col', 'row'))
- output 3: bfloat16 [2, 128, 512, 12, 64], P(None, ('dp', 'col', 'row'))
All inputs are finite; a program needn't handle non-finite values.
Results may differ from a plain program's by a relative error of at most 0.0181874.
Values are sent between devices in bfloat16 or wider.
A program may use at most 1 GiB of HBM per device.

v0:
```python
import functools

import jax
import jax.numpy as jnp
import numpy as np
from jax import lax
from jax.experimental import pallas as pl
from jax.experimental.pallas import tpu as pltpu
from jax.sharding import PartitionSpec as P

NORM_EPS = 1e-6
BUCKET_EDGES = (16, 19, 21, 24, 27, 31, 35, 40, 46, 52, 59, 67, 77, 87, 99, 113)
HEADS = 12
HEAD_DIM = 64
D = HEADS * HEAD_DIM
TOKENS = 2
LANES = 128
HROWS = 16
NEG = -1e30
SEQ_BLOCK = 2
AHEAD = 6
MESH = pl.DeviceIdType.MESH
F32 = jnp.float32
BF16 = jnp.bfloat16
VMEM_LIMIT = 56 << 20


def dot32(a, b):
    return jnp.dot(a, b, preferred_element_type=F32)


def head_mask():
    row = lax.broadcasted_iota(jnp.int32, (HROWS, D), 0)
    col = lax.broadcasted_iota(jnp.int32, (HROWS, D), 1)
    return (col >= row * HEAD_DIM) & (col < (row + 1) * HEAD_DIM)


def spread_query(q_ref, b, seqs, hmask):
    rows = []
    for s in range(TOKENS):
        at = pl.ds(s * seqs + b, 1)
        row = jnp.concatenate([q_ref[0, at, 0:D // 2], q_ref[1, at, 0:D // 2]], axis=1)
        rows.append(jnp.where(hmask, jnp.broadcast_to(row, (HROWS, D)), 0.0))
    return jnp.concatenate(rows, axis=0).astype(BF16)


def softmax_rows(sc):
    top = jnp.max(sc, axis=1, keepdims=True)
    e = jnp.exp(sc - top)
    return (e / jnp.sum(e, axis=1, keepdims=True)).astype(BF16)


def mix_values(probs, vals, hmask, o_ref, b):
    mixed = lax.dot_general(probs, vals, (((1,), (1,)), ((), ())), preferred_element_type=F32)
    for s in range(TOKENS):
        part = jnp.where(hmask, mixed[s * HROWS:(s + 1) * HROWS], 0.0)
        row = jnp.sum(part, axis=0, keepdims=True)
        o_ref[s, pl.ds(b, 1), :] = row.astype(BF16).astype(F32)


def self_kernel(layer, seqs, aliased, pos_ref, qkv_ref, tab_ref, k_in, v_in, *rest):
    k_out, v_out, o_ref, kbuf, vbuf, kvt, in_sem, out_sem = rest[2 if aliased else 0:]
    half = D // 2
    cache_len = kbuf.shape[-1]
    sides = ((0, k_in, k_out, kbuf), (1, v_in, v_out, vbuf))

    def loads(b):
        return [pltpu.make_async_copy(src.at[layer, b], buf.at[b], in_sem.at[n, b]) for n, src, _, buf in sides]

    def stores(b):
        return [pltpu.make_async_copy(buf.at[b], dst.at[layer, b], out_sem.at[n, b]) for n, _, dst, buf in sides]

    for b in range(AHEAD):
        for copy in loads(b):
            copy.start()
    for which in range(2):
        for cb in range(2):
            lo = (which + 1) * half
            kvt[which, pl.ds(cb * half, half), :] = qkv_ref[cb, :, lo:lo + half].T.astype(BF16)

    def step(i, carry):
        hmask = head_mask()
        row_id = lax.broadcasted_iota(jnp.int32, (TOKENS * seqs, LANES), 0)
        lane_id = lax.broadcasted_iota(jnp.int32, (TOKENS * seqs, LANES), 1)
        lane_row = lax.broadcasted_iota(jnp.int32, (D, LANES), 1)
        t_id = lax.broadcasted_iota(jnp.int32, (HROWS, cache_len), 1)
        for j in range(SEQ_BLOCK):
            ahead = i * SEQ_BLOCK + j + AHEAD

            @pl.when(ahead < seqs)
            def _():
                for copy in loads(ahead):
                    copy.start()
        for j in range(SEQ_BLOCK):
            b = i * SEQ_BLOCK + j
            p = pos_ref[b]
            for copy in loads(b):
                copy.wait()
            for s in range(TOKENS):
                t = p + s
                off = pl.multiple_of((t // LANES) * LANES, LANES)
                lane = t - off
                sel = jnp.where((row_id == s * seqs + b) & (lane_id == lane), 1.0, 0.0).astype(BF16)
                here = lane_row == lane
                for n, _, _, buf in sides:
                    ins = dot32(kvt[n], sel)
                    old = buf[b, :, pl.ds(off, LANES)].astype(F32)
                    buf[b, :, pl.ds(off, LANES)] = jnp.where(here, ins, old).astype(BF16)
            for copy in stores(b):
                copy.start()
            qbd = spread_query(qkv_ref, b, seqs, hmask)
            sc = dot32(qbd, kbuf[b])
            parts = []
            for s in range(TOKENS):
                t = p + s
                bias = pltpu.roll(tab_ref[...], lax.rem(t + 1, cache_len), 1)
                parts.append(jnp.where(t_id <= t, sc[s * HROWS:(s + 1) * HROWS] + bias, NEG))
            probs = softmax_rows(jnp.concatenate(parts, axis=0))
            mix_values(probs, vbuf[b], hmask, o_ref, b)
        return carry

    lax.fori_loop(0, seqs // SEQ_BLOCK, step, 0)
    for b in range(seqs):
        for copy in stores(b):
            copy.wait()


def self_attention(layer, pos, qkv, table, cache_k, cache_v, outs):
    layers, seqs, _, cache_len = cache_k.shape
    vm = pl.BlockSpec(memory_space=pltpu.VMEM)
    hb = pl.BlockSpec(memory_space=pl.ANY)
    in_specs = [pl.BlockSpec(memory_space=pltpu.SMEM), vm, vm, hb, hb]
    args = [pos, qkv, table, cache_k, cache_v]
    aliases = {}
    if outs is not None:
        in_specs += [hb, hb]
        args += list(outs)
        aliases = {5: 0, 6: 1}
    buf = pltpu.VMEM((seqs, D, cache_len), BF16)
    return pl.pallas_call(
        functools.partial(self_kernel, layer, seqs, outs is not None),
        out_shape=(jax.ShapeDtypeStruct(cache_k.shape, BF16), jax.ShapeDtypeStruct(cache_v.shape, BF16),
                   jax.ShapeDtypeStruct((TOKENS, seqs, D), F32)),
        in_specs=in_specs,
        out_specs=[hb, hb, vm],
        scratch_shapes=[buf, buf, pltpu.VMEM((2, D, TOKENS * seqs), BF16),
                        pltpu.SemaphoreType.DMA((2, seqs)), pltpu.SemaphoreType.DMA((2, seqs))],
        input_output_aliases=aliases,
        cost_estimate=pl.CostEstimate(flops=20_000_000_000, bytes_accessed=4 * seqs * D * cache_len * 2,
                                      transcendentals=0),
        compiler_params=pltpu.CompilerParams(vmem_limit_bytes=VMEM_LIMIT),
        name="self_attn",
    )(*args)


def rms(res, gain):
    mean_sq = jnp.mean(res * res, axis=-1, keepdims=True)
    return (res * lax.rsqrt(mean_sq + NORM_EPS) * gain.astype(F32)).astype(BF16)


class Stage:
    def __init__(self):
        dp, self.c, self.r = lax.axis_index("dp"), lax.axis_index("col"), lax.axis_index("row")
        self.across = (self.r + 2) % 4
        core = self.r + 1 - 2 * (self.r % 2)
        self.peer = (dp, 1 - self.c, self.r)
        self.partner = (dp, self.c, core)
        self.xpeer = (dp, self.c, self.across)

    def greet(self):
        barrier = pltpu.get_barrier_semaphore()
        for other in (self.peer, self.partner, self.xpeer):
            pl.semaphore_signal(barrier, inc=1, device_id=other, device_id_type=MESH)
        pl.semaphore_wait(barrier, 3)

    def remote(self, src, dst, send_sem, recv_sem, to):
        return pltpu.make_async_remote_copy(src_ref=src, dst_ref=dst, send_sem=send_sem, recv_sem=recv_sem,
                                            device_id=to, device_id_type=MESH)

    def send(self, src, dst, sems):
        copy = self.remote(src, dst, sems.at[0], sems.at[1], self.peer)
        copy.start()
        return copy

    def trade_rows(self, own, buf, sems):
        buf[0] = own
        self.send(buf.at[0], buf.at[1], sems).wait()
        rows, width = own.shape
        return buf[...].reshape(2 * rows, width)

    def trade_columns(self, mine, buf, sems):
        rows, width = mine.shape[0] // 2, mine.shape[1]
        c = self.c
        buf[c] = mine.astype(BF16).reshape(2, rows, width)
        first = self.send(buf.at[c, 0], buf.at[c, 1], sems.at[0])
        second = self.send(buf.at[c, 1], buf.at[c, 0], sems.at[1])
        first.wait()
        second.wait()
        return jnp.concatenate([buf[0].reshape(2 * rows, width), buf[1].reshape(2 * rows, width)], axis=1)

    def give_rows(self, mine, buf, sems, out_ref):
        rows = mine.shape[0] // 2
        c = self.c
        mine = mine.astype(BF16)
        buf[0] = mine[rows:]
        copy = self.send(buf.at[0], buf.at[1], sems)
        out_ref[c] = mine[:rows].astype(F32)
        copy.wait()
        out_ref[1 - c] = buf[1].astype(F32)


class Weight:
    def __init__(self, st, own, dst, col, sems, crossed=None):
        depth, width = own.shape
        self.st, self.crossed = st, crossed

        def place(owner):
            return dst.at[pl.ds(pl.multiple_of(owner * depth, depth), depth), pl.ds(col, width)]

        mine, theirs = place(st.r), place(st.across)
        self.local = pltpu.make_async_copy(own, mine, sems.at[0])
        self.share = st.remote(own, mine, sems.at[1], sems.at[2], st.partner)
        if crossed is None:
            self.cross = st.remote(own, mine, sems.at[3], sems.at[4], st.xpeer)
            self.pass_on = st.remote(theirs, theirs, sems.at[5], sems.at[6], st.partner)
        else:
            self.cross = pltpu.make_async_copy(crossed, theirs, sems.at[3])
            self.pass_on = st.remote(crossed, theirs, sems.at[5], sems.at[6], st.partner)

    def open_local(self):
        self.local.start()
        if self.crossed is not None:
            self.cross.start()

    def open_cross(self):
        if self.crossed is None:
            self.cross.start()

    def open_share(self):
        self.share.start()
        if self.crossed is not None:
            self.pass_on.start()

    def relay(self):
        if self.crossed is None:
            self.cross.wait_recv()
            self.pass_on.start()

    def finish(self):
        self.local.wait()
        self.share.wait()
        if self.crossed is None:
            self.cross.wait_send()
        else:
            self.cross.wait()
        self.pass_on.wait()


def each(items, name):
    for item in items:
        getattr(item, name)()


def weights_of(st, refs, layer, dst, sems, crossed=None):
    col, found = 0, []
    for n, ref in enumerate(refs):
        width = ref.shape[2]
        given = None if crossed is None else crossed.at[:, pl.ds(col, width)]
        found.append(Weight(st, ref.at[layer], dst, col, sems.at[n], given))
        col += width
    return found


def forward(st, refs, layer, dst, sems):
    col, copies = 0, []
    for n, ref in enumerate(refs):
        width = ref.shape[2]
        copies.append(st.remote(ref.at[layer], dst.at[:, pl.ds(col, width)], sems.at[n, 0], sems.at[n, 1], st.xpeer))
        col += width
    return copies


def collect(refs, layer, dst, sems):
    col, copies = 0, []
    for n, ref in enumerate(refs):
        width = ref.shape[2]
        copies.append(pltpu.make_async_copy(ref.at[layer], dst.at[:, pl.ds(col, width)], sems.at[n]))
        col += width
    return copies


def start_kernel(h_ref, gain_ref, wq_r, wk_r, wv_r, wo_r, wc_r, wco_r, wg_r, wu_r,
                 x_ref, qkv_ref, xmid_ref, tail_ref, hbuf, wqkv, qbuf, tbuf, wsem, xsem, tsem, sem):
    st = Stage()
    weights = weights_of(st, (wq_r, wk_r, wv_r), 0, wqkv, wsem)
    middle = forward(st, (wo_r, wc_r), 0, xmid_ref, xsem)
    tail = collect((wco_r, wg_r, wu_r), 0, tbuf, tsem)
    each(weights, "open_local")
    each(tail, "start")
    st.greet()
    each(weights, "open_cross")
    each(middle, "start")
    each(weights, "open_share")
    res = st.trade_rows(h_ref[...], hbuf, sem.at[0]).astype(F32)
    x_ref[...] = res
    normed = rms(res, gain_ref[...])
    each(tail, "wait")
    tail_out = pltpu.make_async_copy(tbuf, tail_ref, tsem.at[3])
    tail_out.start()
    each(weights, "relay")
    each(weights, "finish")
    st.give_rows(dot32(normed, wqkv[...]), qbuf, sem.at[1], qkv_ref)
    tail_out.wait()
    each(middle, "wait")


def layer_kernel(layer, last, seqs, len_ref, o_ref, x_ref, gcross_ref, gmlp_ref, *refs):
    if last:
        (ck, cv, xmid_in, xtail_in, wo_r, wc_r, wco_r, wg_r, wu_r, wd_r, hid_ref,
         kbuf, vbuf, wmid, wtail, wdown, qs, os, obuf, ybuf, qbuf, obuf2, ybuf2, ubuf, zbuf,
         kvsem, msem, wtsem, dsem, sem, sem2) = refs
    else:
        (gself_ref, ck, cv, xmid_in, xtail_in, wo_r, wc_r, wco_r, wg_r, wu_r, wd_r, wq_r, wk_r, wv_r,
         x_out, qkv_ref, xmid_ref, tail_ref,
         kbuf, vbuf, wmid, wtail, wdown, qs, os, obuf, ybuf, qbuf, obuf2, ybuf2, ubuf, zbuf,
         kvsem, msem, wtsem, dsem, sem, sem2, wqkv, qkvbuf, tbuf, wsem, xsem, tsem) = refs
    st = Stage()
    half = D // 2
    rows = o_ref.shape[0]
    mid = weights_of(st, (wo_r, wc_r), layer, wmid, msem, xmid_in)
    tail = weights_of(st, (wco_r, wg_r, wu_r), layer, wtail, wtsem, xtail_in)
    down = weights_of(st, (wd_r,), layer, wdown, dsem)
    each(mid, "open_local")

    def caches(b):
        return [pltpu.make_async_copy(src.at[layer, b], buf.at[b], kvsem.at[n, b])
                for n, (src, buf) in enumerate(((ck, kbuf), (cv, vbuf)))]

    def fetch_caches(b, carry):
        each(caches(b), "start")
        return carry

    lax.fori_loop(0, seqs, fetch_caches, 0)
    each(tail, "open_local")
    each(down, "open_local")
    if not last:
        ahead = weights_of(st, (wq_r, wk_r, wv_r), layer + 1, wqkv, wsem)
        nextmid = forward(st, (wo_r, wc_r), layer + 1, xmid_ref, xsem)
        nexttail = collect((wco_r, wg_r, wu_r), layer + 1, tbuf, tsem)
        each(ahead, "open_local")
        each(nexttail, "start")
    st.greet()
    each(mid, "open_share")
    each(down, "open_cross")
    if not last:
        each(ahead, "open_cross")
        each(nextmid, "start")
    mixed = st.trade_rows(o_ref[...].astype(BF16), obuf, sem.at[0])
    each(mid, "finish")
    y = st.trade_columns(dot32(mixed, wmid[:, 0:half]), ybuf, sem2.at[0])
    res = x_ref[...] + y.astype(F32)
    normed = rms(res, gcross_ref[...])
    st.give_rows(dot32(normed, wmid[:, half:D]), qbuf, sem.at[1], qs)
    each(tail, "open_share")
    each(down, "open_share")
    if not last:
        each(ahead, "open_share")
        each(nexttail, "wait")
        tail_out = pltpu.make_async_copy(tbuf, tail_ref, tsem.at[3])
        tail_out.start()

    def cross_step(i, carry):
        hmask = head_mask()
        t_id = lax.broadcasted_iota(jnp.int32, (TOKENS * HROWS, kbuf.shape[-1]), 1)
        for j in range(SEQ_BLOCK):
            b = i * SEQ_BLOCK + j
            each(caches(b), "wait")
            qbd = spread_query(qs, b, seqs, hmask)
            sc = jnp.where(t_id < len_ref[b], dot32(qbd, kbuf[b]), NEG)
            mix_values(softmax_rows(sc), vbuf[b], hmask, os, b)
        return carry

    lax.fori_loop(0, seqs // SEQ_BLOCK, cross_step, 0)
    each(down, "relay")
    mixed = st.trade_rows(os[...].reshape(rows, D).astype(BF16), obuf2, sem.at[2])
    each(tail, "finish")
    y = st.trade_columns(dot32(mixed, wtail[:, 0:half]), ybuf2, sem2.at[1])
    res = res + y.astype(F32)
    normed = rms(res, gmlp_ref[...])
    ff = (wtail.shape[1] - half) // 2
    gate = dot32(normed, wtail[:, half:half + ff]).astype(BF16).astype(F32)
    up = dot32(normed, wtail[:, half + ff:half + 2 * ff]).astype(BF16).astype(F32)
    act = st.trade_columns(gate * jax.nn.sigmoid(gate) * up, ubuf, sem2.at[2])
    if not last:
        each(ahead, "relay")
    each(down, "finish")
    z = st.trade_columns(dot32(act, wdown[...]), zbuf, sem2.at[3])
    res = res + z.astype(F32)
    if last:
        hid_ref[...] = res[:rows].astype(BF16)
    else:
        x_out[...] = res
        normed = rms(res, gself_ref[...])
        each(ahead, "finish")
        st.give_rows(dot32(normed, wqkv[...]), qkvbuf, sem.at[3], qkv_ref)
        tail_out.wait()
        each(nextmid, "wait")


def exchange_call(kernel, cid, name, specs, args, outs, scratch, flops):
    spaces = {"s": pltpu.SMEM, "v": pltpu.VMEM, "h": pl.ANY}
    spec = lambda letters: [pl.BlockSpec(memory_space=spaces[x]) for x in letters]
    return pl.pallas_call(
        kernel,
        out_shape=tuple(t for _, t in outs),
        in_specs=spec(specs),
        out_specs=tuple(spec(x for x, _ in outs)),
        scratch_shapes=scratch,
        cost_estimate=pl.CostEstimate(flops=flops, bytes_accessed=8 << 20, transcendentals=0),
        compiler_params=pltpu.CompilerParams(collective_id=cid, has_side_effects=True, vmem_limit_bytes=VMEM_LIMIT),
        name=name,
    )(*args)


def bias_table(dec_bias, cache_len):
    dist = np.arange(cache_len)[::-1]
    far = BUCKET_EDGES[0] - 1 + np.sum(dist[:, None] >= np.array(BUCKET_EDGES)[None, :], axis=1)
    bucket = np.where(dist < BUCKET_EDGES[0], dist, far)
    onehot = (np.arange(dec_bias.shape[0])[:, None] == bucket[None, :]).astype(np.float32)
    padded = jnp.pad(dec_bias, ((0, 0), (0, HROWS - dec_bias.shape[1])))
    return lax.dot_general(padded, jnp.asarray(onehot), (((0,), (0,)), ((), ())),
                           precision=lax.Precision.HIGHEST, preferred_element_type=F32)


def solution(mesh):
    batch_axes = ('dp', 'col', 'row')

    def local_step(h_first, h_second, start_pos, enc_lens, dec_bias, norm_self, norm_cross, norm_mlp,
                   w_query, w_key, w_value, w_out, w_cquery, w_cout, w_gate, w_up, w_down,
                   self_k, self_v, cross_k, cross_v):
        layers, seqs, cache_len = self_k.shape[:3]
        rows = TOKENS * seqs
        half = D // 2
        ffc = w_gate.shape[2]
        depth = 4 * w_query.shape[1]
        fdepth = 4 * w_down.shape[1]

        def flat(cache):
            return jnp.transpose(cache, (0, 1, 3, 4, 2)).reshape(layers, seqs, D, cache.shape[2])

        caches = [flat(a) for a in (self_k, self_v, cross_k, cross_v)]
        table = bias_table(dec_bias, cache_len)
        tail_width = half + 2 * ffc
        block = w_query.shape[1]

        vm = lambda shape, dt=BF16: pltpu.VMEM(shape, dt)
        dma = lambda *shape: pltpu.SemaphoreType.DMA(shape)
        rowbuf = lambda width: vm((2, rows, width))
        colbuf = lambda width: vm((2, 2, rows, width))
        res_t = ("v", jax.ShapeDtypeStruct((2 * rows, D), F32))
        qkv_t = ("v", jax.ShapeDtypeStruct((2, rows, 3 * half), F32))
        mid_t = ("h", jax.ShapeDtypeStruct((block, D), BF16))
        tail_t = ("h", jax.ShapeDtypeStruct((block, tail_width), BF16))
        gain = lambda g, l: g[l][None, :]
        across = [(r, (r + 2) % 4) for r in range(4)]

        hidden = jnp.concatenate([h_first, h_second], axis=0)
        res, qkv, xmid, tail_own = exchange_call(
            start_kernel, 0, "start", "vv" + "h" * 8,
            [hidden, gain(norm_self, 0), w_query, w_key, w_value, w_out, w_cquery, w_cout, w_gate, w_up],
            [res_t, qkv_t, mid_t, tail_t],
            [rowbuf(D), vm((depth, 3 * half)), rowbuf(3 * half), vm((block, tail_width)),
             dma(3, 7), dma(2, 2), dma(4), dma(2, 2)], 3_000_000_000)
        outs = None
        for l in range(layers):
            last = l == layers - 1
            xtail = lax.ppermute(tail_own, "row", across)
            k_out, v_out, mixed = self_attention(l, start_pos, qkv, table, caches[0], caches[1], outs)
            outs = (k_out, v_out)
            cache_buf = vm((seqs, D, cross_k.shape[2]))
            scratch = [cache_buf, cache_buf, vm((depth, D)), vm((depth, tail_width)), vm((fdepth, half)),
                       vm((2, rows, half), F32), vm((TOKENS, seqs, D), F32), rowbuf(D), colbuf(half), rowbuf(half),
                       rowbuf(D), colbuf(half), colbuf(ffc), colbuf(half),
                       dma(2, seqs), dma(2, 7), dma(3, 7), dma(1, 7), dma(4, 2), dma(4, 2, 2)]
            args = [enc_lens, mixed.reshape(rows, D), res, gain(norm_cross, l), gain(norm_mlp, l)]
            weights = [caches[2], caches[3], xmid, xtail, w_out, w_cquery, w_cout, w_gate, w_up, w_down]
            if last:
                hid, = exchange_call(
                    functools.partial(layer_kernel, l, True, seqs), 1 + l, "last", "svvvv" + "h" * 10,
                    args + weights, [("v", jax.ShapeDtypeStruct((rows, D), BF16))], scratch, 20_000_000_000)
            else:
                scratch += [vm((depth, 3 * half)), rowbuf(3 * half), vm((block, tail_width)),
                            dma(3, 7), dma(2, 2), dma(4)]
                res, qkv, xmid, tail_own = exchange_call(
                    functools.partial(layer_kernel, l, False, seqs), 1 + l, "layer", "svvvvv" + "h" * 13,
                    args + [gain(norm_self, l + 1)] + weights + [w_query, w_key, w_value],
                    [res_t, qkv_t, mid_t, tail_t], scratch, 20_000_000_000)

        def unflat(cache):
            return jnp.transpose(cache.reshape(layers, seqs, HEADS, HEAD_DIM, cache_len), (0, 1, 4, 2, 3))

        return hid.reshape(TOKENS, seqs, D), unflat(outs[0]), unflat(outs[1])

    row_spec = P(batch_axes, None)
    seq_spec = P(batch_axes)
    weight_spec = P(None, 'row', 'col')
    cache_spec = P(None, batch_axes)
    in_specs = (row_spec, row_spec, seq_spec, seq_spec, P(), P(), P(), P()) + (weight_spec,) * 9 + (cache_spec,) * 4
    out_specs = (P(None, batch_axes), cache_spec, cache_spec)
    return jax.shard_map(local_step, mesh=mesh, in_specs=in_specs, out_specs=out_specs, check_vma=False)
```

profile of v0, /device:TPU:0, one launch (start us, length us, event | category | flops | bytes accessed | tf_op | source)
XLA Modules:
  0.0 167.5 jit_solution(5505016112844665957)
XLA Ops:
  0.6 1.4 fusion.5
  2.0 1.4 pad_maximum_fusion.h_ref
  3.4 22.9 %start.1 = (f32[64,768]{1,0:T(8,128)}, f32[2,32,1152]{2,1,0:T(8,128)}, bf16[192,768]{1,0:T(8,128)(2,1)}, bf16[192,2432]{1,0:T(8,128)(2,1)}) custom-call(bf16[32,768]{1,0:T(8,128)(2,1)} %pad_maximum_fusion.h_ref, bf16[1,768]{1,0:T(2,128)(2,1)} %get-tuple-element.36.gain_ref, bf16[2,192,384]{2,1,0:T(8,128)(2,1)} %refs_11_.1, bf16[2,192,384]{2,1,0:T(8,128)(2,1)} %refs_12_.1, ...), custom_call_target="tpu_custom_call" | custom-call | flops 3000000000 | bytes 8388608 | tf_op jit(solution)/shard_map/start/pallas_call | solution.py:413
  26.3 1.1 collective-permute-start
  27.4 1.6 fusion.tab_ref
  29.1 0.0 copy-start
  29.1 0.0 copy-start.1
  29.1 22.2 %self_attn.2 = (bf16[2,16,768,512]{3,2,1,0:T(8,128)(2,1)}, bf16[2,16,768,512]{3,2,1,0:T(8,128)(2,1)}, f32[2,16,768]{2,1,0:T(8,128)}) custom-call(s32[16]{0:T(128)} %pos_ref.3, f32[2,32,1152]{2,1,0:T(8,128)} %get-tuple-element.17.qkv_ref, f32[16,512]{1,0:T(8,128)} %fusion.tab_ref, bf16[2,16,768,512]{3,2,1,0:T(8,128)(2,1)} %bitcast.22, ...), custom_call_target="tpu_custom_call" | custom-call | flops 20000000000 | bytes 50331648 | tf_op jit(solution)/shard_map/self_attn/pallas_call | solution.py:140
  51.3 0.0 copy-done
  51.3 0.0 copy-done.1
  51.3 0.6 fusion.3
  51.9 0.0 collective-permute-done.refs_4_
  51.9 0.0 copy-start.2
  51.9 1.0 copy-done.2
  52.9 46.6 %layer.1 = (f32[64,768]{1,0:T(8,128)}, f32[2,32,1152]{2,1,0:T(8,128)}, bf16[192,768]{1,0:T(8,128)(2,1)}, bf16[192,2432]{1,0:T(8,128)(2,1)}) custom-call(s32[16]{0:T(128)} %len_ref.3, f32[32,768]{1,0:T(8,128)} %bitcast.34, f32[64,768]{1,0:T(8,128)} %get-tuple-element.19.x_ref, bf16[1,768]{1,0:T(2,128)(2,1)} %get-tuple-element.37.gcross_ref, ...), custom_call_target="tpu_custom_call" | custom-call | flops 20000000000 | bytes 8388608 | tf_op jit(solution)/shard_map/layer/pallas_call | solution.py:413
  99.5 1.4 collective-permute-start.1
  100.9 22.2 %self_attn.3 = (bf16[2,16,768,512]{3,2,1,0:T(8,128)(2,1)}, bf16[2,16,768,512]{3,2,1,0:T(8,128)(2,1)}, f32[2,16,768]{2,1,0:T(8,128)}) custom-call(s32[16]{0:T(128)} %pos_ref.3, f32[2,32,1152]{2,1,0:T(8,128)} %get-tuple-element.22.qkv_ref, f32[16,512]{1,0:T(8,128)} %fusion.tab_ref, ...), custom_call_target="tpu_custom_call", output_to_operand_aliasing={{0}: (5, {}), {1}: (6, {})} | custom-call | flops 20000000000 | bytes 50331648 | tf_op jit(solution)/shard_map/self_attn/pallas_call | solution.py:140
  123.1 0.0 collective-permute-done.1.refs_3_
  123.1 0.0 copy-start.3
  123.1 0.9 copy-done.3
  124.0 42.1 %last.1 = bf16[32,768]{1,0:T(8,128)(2,1)} custom-call(s32[16]{0:T(128)} %len_ref.3, f32[32,768]{1,0:T(8,128)} %bitcast.33, f32[64,768]{1,0:T(8,128)} %get-tuple-element.26.x_ref, bf16[1,768]{1,0:T(2,128)(2,1)} %get-tuple-element.38.gcross_ref, bf16[1,768]{1,0:T(2,128)(2,1)} %get-tuple-element.31.gmlp_ref, bf16[2,16,768,512]{3,2,1,0:T(8,128)(2,1)} %bitcast.30, ...), custom_call_target="tpu_custom_call" | custom-call | flops 20000000000 | bytes 8388608 | tf_op jit(solution)/shard_map/last/pallas_call | solution.py:413
  166.1 1.4 copy.30
Async XLA Ops:
  26.3 25.6 %collective-permute-start = (bf16[192,2432]{1,0:T(8,128)(2,1)}, bf16[192,2432]{1,0:T(8,128)(2,1)S(1)}, u32[]{:S(2)}, u32[]{:S(2)}) collective-permute-start(bf16[192,2432]{1,0:T(8,128)(2,1)} %get-tuple-element.21), channel_id=1, source_target_pairs={{0,2},{1,3},{2,0},{3,1},{4,6},{5,7},{6,4},{7,5}} | collective-permute-start | bytes 2801672 | tf_op jit(solution)/shard_map/ppermute | solution.py:477
  29.1 22.2 %copy-start = (bf16[2,768]{1,0:T(2,128)(2,1)S(1)}, bf16[2,768]{1,0:T(2,128)(2,1)}, u32[]{:S(2)}) copy-start(bf16[2,768]{1,0:T(2,128)(2,1)} %param.29) | copy-start | bytes 9220
  29.1 22.2 %copy-start.1 = (bf16[2,768]{1,0:T(2,128)(2,1)S(1)}, bf16[2,768]{1,0:T(2,128)(2,1)}, u32[]{:S(2)}) copy-start(bf16[2,768]{1,0:T(2,128)(2,1)} %param.28) | copy-start | bytes 9220
  51.9 1.0 copy-start.2
  99.5 23.5 %collective-permute-start.1 = (bf16[192,2432]{1,0:T(8,128)(2,1)}, bf16[192,2432]{1,0:T(8,128)(2,1)S(1)}, u32[]{:S(2)}, u32[]{:S(2)}) collective-permute-start(bf16[192,2432]{1,0:T(8,128)(2,1)} %get-tuple-element.28), channel_id=1, source_target_pairs={{0,2},{1,3},{2,0},{3,1},{4,6},{5,7},{6,4},{7,5}} | collective-permute-start | bytes 2801672 | tf_op jit(solution)/shard_map/ppermute | solution.py:477
  123.1 0.9 copy-start.3
where the time goes:
time: 168 us
  Pallas kernels  156 us (93%)
  local copies, waits for them, and re-layouts  5.31 us (3%)
  starting transfers between devices  2.48 us (1%)
    pallas_call x3, Pallas kernels, exchange_call(): pl.pallas_call(kernel, out_shape=tuple((t for _, t in outs)), in_specs=sp...  112 us
    pallas_call x2, Pallas kernels, self_attention(): pl.pallas_call(functools.partial(self_kernel, layer, seqs, outs is not No...  44.3 us
  transfers between devices with their start and end apart: 2, of which 0 were waited for; matrix products, arithmetic and copies ran while one was open for 1% of the time, Pallas kernels for 26%

commit v1 on v0

--- a/solution.py
+++ b/solution.py
@@ -17,12 +17,12 @@
 LANES = 128
 HROWS = 16
 NEG = -1e30
-SEQ_BLOCK = 2
-AHEAD = 6
+SEQ_BLOCK = 4
+AHEAD = 8
 MESH = pl.DeviceIdType.MESH
 F32 = jnp.float32
 BF16 = jnp.bfloat16
-VMEM_LIMIT = 56 << 20
+VMEM_LIMIT = 67_043_328
 
 
 def dot32(a, b):
@@ -50,12 +50,15 @@
     return (e / jnp.sum(e, axis=1, keepdims=True)).astype(BF16)
 
 
-def mix_values(probs, vals, hmask, o_ref, b):
-    mixed = lax.dot_general(probs, vals, (((1,), (1,)), ((), ())), preferred_element_type=F32)
-    for s in range(TOKENS):
-        part = jnp.where(hmask, mixed[s * HROWS:(s + 1) * HROWS], 0.0)
-        row = jnp.sum(part, axis=0, keepdims=True)
-        o_ref[s, pl.ds(b, 1), :] = row.astype(BF16).astype(F32)
+def mix_values(probs, values, seqids, hmask, o_ref):
+    group = TOKENS * HROWS
+    mixes = [lax.dot_general(probs[n * group:(n + 1) * group], values[b], (((1,), (1,)), ((), ())),
+                             preferred_element_type=F32) for n, b in enumerate(seqids)]
+    for b, mixed in zip(seqids, mixes):
+        for s in range(TOKENS):
+            part = jnp.where(hmask, mixed[s * HROWS:(s + 1) * HROWS], 0.0)
+            row = jnp.sum(part, axis=0, keepdims=True)
+            o_ref[s, pl.ds(b, 1), :] = row.astype(BF16).astype(F32)
 
 
 def self_kernel(layer, seqs, aliased, pos_ref, qkv_ref, tab_ref, k_in, v_in, *rest):
@@ -80,43 +83,44 @@
 
     def step(i, carry):
         hmask = head_mask()
-        row_id = lax.broadcasted_iota(jnp.int32, (TOKENS * seqs, LANES), 0)
-        lane_id = lax.broadcasted_iota(jnp.int32, (TOKENS * seqs, LANES), 1)
-        lane_row = lax.broadcasted_iota(jnp.int32, (D, LANES), 1)
+        wide = 2 * LANES
+        row_id = lax.broadcasted_iota(jnp.int32, (TOKENS * seqs, wide), 0)
+        lane_id = lax.broadcasted_iota(jnp.int32, (TOKENS * seqs, wide), 1)
+        lane_row = lax.broadcasted_iota(jnp.int32, (D, wide), 1)
         t_id = lax.broadcasted_iota(jnp.int32, (HROWS, cache_len), 1)
-        for j in range(SEQ_BLOCK):
-            ahead = i * SEQ_BLOCK + j + AHEAD
+        seqids = [i * SEQ_BLOCK + j for j in range(SEQ_BLOCK)]
+        for b in seqids:
+            ahead = b + AHEAD
 
             @pl.when(ahead < seqs)
             def _():
                 for copy in loads(ahead):
                     copy.start()
-        for j in range(SEQ_BLOCK):
-            b = i * SEQ_BLOCK + j
-            p = pos_ref[b]
+        for b in seqids:
             for copy in loads(b):
                 copy.wait()
-            for s in range(TOKENS):
-                t = p + s
-                off = pl.multiple_of((t // LANES) * LANES, LANES)
-                lane = t - off
-                sel = jnp.where((row_id == s * seqs + b) & (lane_id == lane), 1.0, 0.0).astype(BF16)
-                here = lane_row == lane
-                for n, _, _, buf in sides:
-                    ins = dot32(kvt[n], sel)
-                    old = buf[b, :, pl.ds(off, LANES)].astype(F32)
-                    buf[b, :, pl.ds(off, LANES)] = jnp.where(here, ins, old).astype(BF16)
+        for b in seqids:
+            p = pos_ref[b]
+            off = pl.multiple_of(jnp.minimum(p // LANES, cache_len // LANES - 2) * LANES, LANES)
+            lane = p - off
+            sel = ((row_id == b) & (lane_id == lane)) | ((row_id == seqs + b) & (lane_id == lane + 1))
+            sel = jnp.where(sel, 1.0, 0.0).astype(BF16)
+            here = (lane_row == lane) | (lane_row == lane + 1)
+            for n, _, _, buf in sides:
+                ins = dot32(kvt[n], sel)
+                old = buf[b, :, pl.ds(off, wide)].astype(F32)
+                buf[b, :, pl.ds(off, wide)] = jnp.where(here, ins, old).astype(BF16)
             for copy in stores(b):
                 copy.start()
-            qbd = spread_query(qkv_ref, b, seqs, hmask)
-            sc = dot32(qbd, kbuf[b])
-            parts = []
+        queries = [spread_query(qkv_ref, b, seqs, hmask) for b in seqids]
+        scores = [dot32(q, kbuf[b]) for q, b in zip(queries, seqids)]
+        parts = []
+        for b, sc in zip(seqids, scores):
             for s in range(TOKENS):
-                t = p + s
+                t = pos_ref[b] + s
                 bias = pltpu.roll(tab_ref[...], lax.rem(t + 1, cache_len), 1)
                 parts.append(jnp.where(t_id <= t, sc[s * HROWS:(s + 1) * HROWS] + bias, NEG))
-            probs = softmax_rows(jnp.concatenate(parts, axis=0))
-            mix_values(probs, vbuf[b], hmask, o_ref, b)
+        mix_values(softmax_rows(jnp.concatenate(parts, axis=0)), vbuf, seqids, hmask, o_ref)
         return carry
 
     lax.fori_loop(0, seqs // SEQ_BLOCK, step, 0)
@@ -185,8 +189,7 @@
     def trade_rows(self, own, buf, sems):
         buf[0] = own
         self.send(buf.at[0], buf.at[1], sems).wait()
-        rows, width = own.shape
-        return buf[...].reshape(2 * rows, width)
+        return jnp.concatenate([buf[0], buf[1]], axis=0)
 
     def trade_columns(self, mine, buf, sems):
         rows, width = mine.shape[0] // 2, mine.shape[1]
@@ -289,48 +292,85 @@
     return copies
 
 
+class Whole:
+    def __init__(self, st, packs, dst, sems):
+        block = packs[0].shape[1]
+        self.locals, self.shares = [], []
+        for n, (pack, cb) in enumerate(zip(packs, (st.c, 1 - st.c))):
+            for m, owner in enumerate((st.r, st.across)):
+                place = dst.at[cb, pl.ds(pl.multiple_of(owner * block, block), block), :]
+                self.locals.append(pltpu.make_async_copy(pack.at[m], place, sems.at[n, m, 0]))
+                self.shares.append(st.remote(pack.at[m], place, sems.at[n, m, 1], sems.at[n, m, 2], st.partner))
+
+    def open_local(self):
+        each(self.locals, "start")
+
+    def open_share(self):
+        each(self.shares, "start")
+
+    def finish(self):
+        each(self.locals, "wait")
+        each(self.shares, "wait")
+
+
+class NextLayer:
+    def __init__(self, st, attn, mlp, layer, pack_ref, tail_ref, pbuf, tbuf, sems, xsems):
+        self.loads = collect(attn, layer, pbuf, sems.at[0]) + collect(mlp, layer, tbuf, sems.at[1])
+        self.sends = forward(st, attn, layer, pack_ref.at[1], xsems)
+        self.stores = [pltpu.make_async_copy(pbuf, pack_ref.at[0], sems.at[2, 0]),
+                       pltpu.make_async_copy(tbuf, tail_ref, sems.at[2, 1])]
+
+    def store(self):
+        each(self.loads, "wait")
+        each(self.stores, "start")
+
+    def finish(self):
+        each(self.stores, "wait")
+        each(self.sends, "wait")
+
+
 def start_kernel(h_ref, gain_ref, wq_r, wk_r, wv_r, wo_r, wc_r, wco_r, wg_r, wu_r,
-                 x_ref, qkv_ref, xmid_ref, tail_ref, hbuf, wqkv, qbuf, tbuf, wsem, xsem, tsem, sem):
+                 x_ref, qkv_ref, pack_ref, tail_ref, hbuf, wqkv, qbuf, pbuf, tbuf, wsem, nsem, xsem, sem):
     st = Stage()
     weights = weights_of(st, (wq_r, wk_r, wv_r), 0, wqkv, wsem)
-    middle = forward(st, (wo_r, wc_r), 0, xmid_ref, xsem)
-    tail = collect((wco_r, wg_r, wu_r), 0, tbuf, tsem)
+    coming = NextLayer(st, (wo_r, wc_r, wco_r), (wg_r, wu_r), 0, pack_ref, tail_ref, pbuf, tbuf, nsem, xsem)
     each(weights, "open_local")
-    each(tail, "start")
+    each(coming.loads, "start")
     st.greet()
     each(weights, "open_cross")
-    each(middle, "start")
+    each(coming.sends, "start")
     each(weights, "open_share")
     res = st.trade_rows(h_ref[...], hbuf, sem.at[0]).astype(F32)
-    x_ref[...] = res
+    x_ref[...] = res[:h_ref.shape[0]]
     normed = rms(res, gain_ref[...])
-    each(tail, "wait")
-    tail_out = pltpu.make_async_copy(tbuf, tail_ref, tsem.at[3])
-    tail_out.start()
+    coming.store()
     each(weights, "relay")
     each(weights, "finish")
     st.give_rows(dot32(normed, wqkv[...]), qbuf, sem.at[1], qkv_ref)
-    tail_out.wait()
-    each(middle, "wait")
+    coming.finish()
+
+
+def both_blocks(act, packed, which):
+    half = D // 2
+    cols = slice(which * half, (which + 1) * half)
+    return [dot32(act, packed[cb, :, cols]).astype(BF16) for cb in range(2)]
 
 
 def layer_kernel(layer, last, seqs, len_ref, o_ref, x_ref, gcross_ref, gmlp_ref, *refs):
     if last:
-        (ck, cv, xmid_in, xtail_in, wo_r, wc_r, wco_r, wg_r, wu_r, wd_r, hid_ref,
-         kbuf, vbuf, wmid, wtail, wdown, qs, os, obuf, ybuf, qbuf, obuf2, ybuf2, ubuf, zbuf,
-         kvsem, msem, wtsem, dsem, sem, sem2) = refs
+        (ck, cv, pack_in, ypack_in, xtail_in, wg_r, wu_r, wd_r, hid_ref,
+         kbuf, vbuf, wattn, wtail, wdown, qs, os, ubuf, kvsem, asem, wtsem, dsem, sem, sem2, nbuf, zbuf, zs) = refs
     else:
-        (gself_ref, ck, cv, xmid_in, xtail_in, wo_r, wc_r, wco_r, wg_r, wu_r, wd_r, wq_r, wk_r, wv_r,
-         x_out, qkv_ref, xmid_ref, tail_ref,
-         kbuf, vbuf, wmid, wtail, wdown, qs, os, obuf, ybuf, qbuf, obuf2, ybuf2, ubuf, zbuf,
-         kvsem, msem, wtsem, dsem, sem, sem2, wqkv, qkvbuf, tbuf, wsem, xsem, tsem) = refs
+        (gself_ref, ck, cv, pack_in, ypack_in, xtail_in, wg_r, wu_r, wd_r, wq_r, wk_r, wv_r, wo_r, wc_r, wco_r,
+         x_out, qkv_ref, pack_ref, tail_ref,
+         kbuf, vbuf, wattn, wtail, wdown, qs, os, ubuf, kvsem, asem, wtsem, dsem, sem, sem2,
+         rbuf, zbuf, wqkv, qkvbuf, pbuf, tbuf, wsem, nsem, xsem) = refs
     st = Stage()
-    half = D // 2
     rows = o_ref.shape[0]
-    mid = weights_of(st, (wo_r, wc_r), layer, wmid, msem, xmid_in)
-    tail = weights_of(st, (wco_r, wg_r, wu_r), layer, wtail, wtsem, xtail_in)
+    attn = Whole(st, (pack_in, ypack_in), wattn, asem)
+    tail = weights_of(st, (wg_r, wu_r), layer, wtail, wtsem, xtail_in)
     down = weights_of(st, (wd_r,), layer, wdown, dsem)
-    each(mid, "open_local")
+    attn.open_local()
 
     def caches(b):
         return [pltpu.make_async_copy(src.at[layer, b], buf.at[b], kvsem.at[n, b])
@@ -340,71 +380,71 @@
         each(caches(b), "start")
         return carry
 
+    st.greet()
+    attn.open_share()
+    each(down, "open_cross")
     lax.fori_loop(0, seqs, fetch_caches, 0)
     each(tail, "open_local")
     each(down, "open_local")
     if not last:
         ahead = weights_of(st, (wq_r, wk_r, wv_r), layer + 1, wqkv, wsem)
-        nextmid = forward(st, (wo_r, wc_r), layer + 1, xmid_ref, xsem)
-        nexttail = collect((wco_r, wg_r, wu_r), layer + 1, tbuf, tsem)
+        coming = NextLayer(st, (wo_r, wc_r, wco_r), (wg_r, wu_r), layer + 1, pack_ref, tail_ref, pbuf, tbuf,
+                           nsem, xsem)
+        each(ahead, "open_cross")
+        each(coming.sends, "start")
         each(ahead, "open_local")
-        each(nexttail, "start")
-    st.greet()
-    each(mid, "open_share")
-    each(down, "open_cross")
-    if not last:
-        each(ahead, "open_cross")
-        each(nextmid, "start")
-    mixed = st.trade_rows(o_ref[...].astype(BF16), obuf, sem.at[0])
-    each(mid, "finish")
-    y = st.trade_columns(dot32(mixed, wmid[:, 0:half]), ybuf, sem2.at[0])
+        each(coming.loads, "start")
+    attn.finish()
+    y = jnp.concatenate(both_blocks(o_ref[...].astype(BF16), wattn, 0), axis=1)
     res = x_ref[...] + y.astype(F32)
-    normed = rms(res, gcross_ref[...])
-    st.give_rows(dot32(normed, wmid[:, half:D]), qbuf, sem.at[1], qs)
+    for cb, q in enumerate(both_blocks(rms(res, gcross_ref[...]), wattn, 1)):
+        qs[cb] = q.astype(F32)
     each(tail, "open_share")
     each(down, "open_share")
     if not last:
         each(ahead, "open_share")
-        each(nexttail, "wait")
-        tail_out = pltpu.make_async_copy(tbuf, tail_ref, tsem.at[3])
-        tail_out.start()
+        coming.store()
 
     def cross_step(i, carry):
         hmask = head_mask()
         t_id = lax.broadcasted_iota(jnp.int32, (TOKENS * HROWS, kbuf.shape[-1]), 1)
-        for j in range(SEQ_BLOCK):
-            b = i * SEQ_BLOCK + j
+        seqids = [i * SEQ_BLOCK + j for j in range(SEQ_BLOCK)]
+        for b in seqids:
             each(caches(b), "wait")
-            qbd = spread_query(qs, b, seqs, hmask)
-            sc = jnp.where(t_id < len_ref[b], dot32(qbd, kbuf[b]), NEG)
-            mix_values(softmax_rows(sc), vbuf[b], hmask, os, b)
+        queries = [spread_query(qs, b, seqs, hmask) for b in seqids]
+        scores = [dot32(q, kbuf[b]) for q, b in zip(queries, seqids)]
+        parts = [jnp.where(t_id < len_ref[b], sc, NEG) for b, sc in zip(seqids, scores)]
+        mix_values(softmax_rows(jnp.concatenate(parts, axis=0)), vbuf, seqids, hmask, os)
         return carry
 
     lax.fori_loop(0, seqs // SEQ_BLOCK, cross_step, 0)
     each(down, "relay")
-    mixed = st.trade_rows(os[...].reshape(rows, D).astype(BF16), obuf2, sem.at[2])
+    y = jnp.concatenate(both_blocks(os[...].reshape(rows, D).astype(BF16), wattn, 2), axis=1)
+    res = res + y.astype(F32)
+    if last:
+        normed = st.trade_rows(rms(res, gmlp_ref[...]), nbuf, sem.at[0])
+    else:
+        res = st.trade_rows(res, rbuf, sem.at[0])
+        normed = rms(res, gmlp_ref[...])
     each(tail, "finish")
-    y = st.trade_columns(dot32(mixed, wtail[:, 0:half]), ybuf2, sem2.at[1])
-    res = res + y.astype(F32)
-    normed = rms(res, gmlp_ref[...])
-    ff = (wtail.shape[1] - half) // 2
-    gate = dot32(normed, wtail[:, half:half + ff]).astype(BF16).astype(F32)
-    up = dot32(normed, wtail[:, half + ff:half + 2 * ff]).astype(BF16).astype(F32)
-    act = st.trade_columns(gate * jax.nn.sigmoid(gate) * up, ubuf, sem2.at[2])
+    ff = wtail.shape[1] // 2
+    gate = dot32(normed, wtail[:, 0:ff]).astype(BF16).astype(F32)
+    up = dot32(normed, wtail[:, ff:2 * ff]).astype(BF16).astype(F32)
+    act = st.trade_columns(gate * jax.nn.sigmoid(gate) * up, ubuf, sem2.at[0])
     if not last:
         each(ahead, "relay")
     each(down, "finish")
-    z = st.trade_columns(dot32(act, wdown[...]), zbuf, sem2.at[3])
-    res = res + z.astype(F32)
+    z = dot32(act, wdown[...])
     if last:
-        hid_ref[...] = res[:rows].astype(BF16)
+        st.give_rows(z, zbuf, sem.at[1], zs)
+        hid_ref[...] = (res + jnp.concatenate([zs[0], zs[1]], axis=1)).astype(BF16)
     else:
-        x_out[...] = res
+        res = res + st.trade_columns(z, zbuf, sem2.at[1]).astype(F32)
+        x_out[...] = res[:rows]
         normed = rms(res, gself_ref[...])
         each(ahead, "finish")
-        st.give_rows(dot32(normed, wqkv[...]), qkvbuf, sem.at[3], qkv_ref)
-        tail_out.wait()
-        each(nextmid, "wait")
+        st.give_rows(dot32(normed, wqkv[...]), qkvbuf, sem.at[1], qkv_ref)
+        coming.finish()
 
 
 def exchange_call(kernel, cid, name, specs, args, outs, scratch, flops):
@@ -450,51 +490,54 @@
 
         caches = [flat(a) for a in (self_k, self_v, cross_k, cross_v)]
         table = bias_table(dec_bias, cache_len)
-        tail_width = half + 2 * ffc
         block = w_query.shape[1]
 
         vm = lambda shape, dt=BF16: pltpu.VMEM(shape, dt)
         dma = lambda *shape: pltpu.SemaphoreType.DMA(shape)
-        rowbuf = lambda width: vm((2, rows, width))
+        rowbuf = lambda width, dt=BF16: vm((2, rows, width), dt)
         colbuf = lambda width: vm((2, 2, rows, width))
-        res_t = ("v", jax.ShapeDtypeStruct((2 * rows, D), F32))
+        res_t = ("v", jax.ShapeDtypeStruct((rows, D), F32))
         qkv_t = ("v", jax.ShapeDtypeStruct((2, rows, 3 * half), F32))
-        mid_t = ("h", jax.ShapeDtypeStruct((block, D), BF16))
-        tail_t = ("h", jax.ShapeDtypeStruct((block, tail_width), BF16))
+        pack_t = ("h", jax.ShapeDtypeStruct((2, block, 3 * half), BF16))
+        tail_t = ("h", jax.ShapeDtypeStruct((block, 2 * ffc), BF16))
+        coming = [vm((block, 3 * half)), vm((block, 2 * ffc))]
         gain = lambda g, l: g[l][None, :]
         across = [(r, (r + 2) % 4) for r in range(4)]
+        flip = [(0, 1), (1, 0)]
 
         hidden = jnp.concatenate([h_first, h_second], axis=0)
-        res, qkv, xmid, tail_own = exchange_call(
+        res, qkv, pack, tail_own = exchange_call(
             start_kernel, 0, "start", "vv" + "h" * 8,
             [hidden, gain(norm_self, 0), w_query, w_key, w_value, w_out, w_cquery, w_cout, w_gate, w_up],
-            [res_t, qkv_t, mid_t, tail_t],
-            [rowbuf(D), vm((depth, 3 * half)), rowbuf(3 * half), vm((block, tail_width)),
-             dma(3, 7), dma(2, 2), dma(4), dma(2, 2)], 3_000_000_000)
+            [res_t, qkv_t, pack_t, tail_t],
+            [rowbuf(D), vm((depth, 3 * half)), rowbuf(3 * half)] + coming
+            + [dma(3, 7), dma(3, 3), dma(3, 2), dma(2, 2)], 3_000_000_000)
         outs = None
         for l in range(layers):
             last = l == layers - 1
+            ypack = lax.ppermute(pack, "col", flip)
             xtail = lax.ppermute(tail_own, "row", across)
             k_out, v_out, mixed = self_attention(l, start_pos, qkv, table, caches[0], caches[1], outs)
             outs = (k_out, v_out)
             cache_buf = vm((seqs, D, cross_k.shape[2]))
-            scratch = [cache_buf, cache_buf, vm((depth, D)), vm((depth, tail_width)), vm((fdepth, half)),
-                       vm((2, rows, half), F32), vm((TOKENS, seqs, D), F32), rowbuf(D), colbuf(half), rowbuf(half),
-                       rowbuf(D), colbuf(half), colbuf(ffc), colbuf(half),
-                       dma(2, seqs), dma(2, 7), dma(3, 7), dma(1, 7), dma(4, 2), dma(4, 2, 2)]
+            scratch = [cache_buf, cache_buf, vm((2, depth, 3 * half)), vm((depth, 2 * ffc)), vm((fdepth, half)),
+                       vm((2, rows, half), F32), vm((TOKENS, seqs, D), F32), colbuf(ffc),
+                       dma(2, seqs), dma(2, 2, 3), dma(2, 7), dma(1, 7), dma(2, 2), dma(2, 2, 2)]
             args = [enc_lens, mixed.reshape(rows, D), res, gain(norm_cross, l), gain(norm_mlp, l)]
-            weights = [caches[2], caches[3], xmid, xtail, w_out, w_cquery, w_cout, w_gate, w_up, w_down]
+            weights = [caches[2], caches[3], pack, ypack, xtail, w_gate, w_up, w_down]
             if last:
                 hid, = exchange_call(
-                    functools.partial(layer_kernel, l, True, seqs), 1 + l, "last", "svvvv" + "h" * 10,
-                    args + weights, [("v", jax.ShapeDtypeStruct((rows, D), BF16))], scratch, 20_000_000_000)
+                    functools.partial(layer_kernel, l, True, seqs), 1 + l, "last", "svvvv" + "h" * 8,
+                    args + weights, [("v", jax.ShapeDtypeStruct((rows, D), BF16))],
+                    scratch + [rowbuf(D), rowbuf(half), vm((2, rows, half), F32)], 20_000_000_000)
             else:
-                scratch += [vm((depth, 3 * half)), rowbuf(3 * half), vm((block, tail_width)),
-                            dma(3, 7), dma(2, 2), dma(4)]
-                res, qkv, xmid, tail_own = exchange_call(
-                    functools.partial(layer_kernel, l, False, seqs), 1 + l, "layer", "svvvvv" + "h" * 13,
-                    args + [gain(norm_self, l + 1)] + weights + [w_query, w_key, w_value],
-                    [res_t, qkv_t, mid_t, tail_t], scratch, 20_000_000_000)
+                scratch += [rowbuf(D, F32), colbuf(half), vm((depth, 3 * half)), rowbuf(3 * half)] + coming
+                scratch += [dma(3, 7), dma(3, 3), dma(3, 2)]
+                res, qkv, pack, tail_own = exchange_call(
+                    functools.partial(layer_kernel, l, False, seqs), 1 + l, "layer", "svvvvv" + "h" * 14,
+                    args + [gain(norm_self, l + 1)] + weights
+                    + [w_query, w_key, w_value, w_out, w_cquery, w_cout],
+                    [res_t, qkv_t, pack_t, tail_t], scratch, 20_000_000_000)
 
         def unflat(cache):
             return jnp.transpose(cache.reshape(layers, seqs, HEADS, HEAD_DIM, cache_len), (0, 1, 4, 2, 3))

time: 168 us -> 138 us (0.82)
  Pallas kernels: 156 us -> 126 us
    pallas_call x3, Pallas kernels: 112 us -> 87.5 us  [exchange_call(): pl.pallas_call(kernel, out_shape=tuple((t for _, t in outs)), in_specs=sp...]
    pallas_call x2, Pallas kernels: 44.3 us -> 38.1 us  [self_attention(): pl.pallas_call(functools.partial(self_kernel, layer, seqs, outs is not No...]
    ppermute x0 -> x2, starting transfers between devices: none -> 2.46 us  [local_step(): ypack = lax.ppermute(pack, 'col', flip)]
    unnamed x9 -> x1, local copies, waits for them, and re-layouts: 3.34 us -> 1.42 us
  transfers between devices with their start and end apart: 2 -> 4, of which waited for: 0 -> 0; matrix products, arithmetic and copies ran while one was open for 1% -> 2% of each run, Pallas kernels for 26% -> 28%
where the time goes in v1:
time: 138 us
  Pallas kernels  126 us (91%)
  local copies, waits for them, and re-layouts  4.16 us (3%)
  starting transfers between devices  4.09 us (3%)
  matrix products  1.64 us (1%)
    pallas_call x3, Pallas kernels, exchange_call(): pl.pallas_call(kernel, out_shape=tuple((t for _, t in outs)), in_specs=sp...  87.5 us
    pallas_call x2, Pallas kernels, self_attention(): pl.pallas_call(functools.partial(self_kernel, layer, seqs, outs is not No...  38.1 us
  transfers between devices with their start and end apart: 4, of which 0 were waited for; matrix products, arithmetic and copies ran while one was open for 2% of the time, Pallas kernels for 28%

profile of v1, /device:TPU:0, one launch (start us, length us, event | category | flops | bytes accessed | tf_op | source)
XLA Modules:
  0.0 137.6 jit_solution(9889567108972662854)
XLA Ops:
  0.6 1.4 fusion.5
  2.0 1.4 %pad_maximum_fusion.h_ref = bf16[32,768]{1,0:T(8,128)(2,1)} fusion(bf16[16,768]{1,0:T(8,128)(2,1)} %param.23, bf16[16,768]{1,0:T(8,128)(2,1)} %param.22), kind=kLoop, calls=%fused_computation | loop fusion | flops 98304 | bytes 98304 | tf_op jit(solution)/shard_map/concatenate | solution.py:508
  3.4 26.1 %start.1 = (f32[32,768]{1,0:T(8,128)}, f32[2,32,1152]{2,1,0:T(8,128)}, bf16[2,192,1152]{2,1,0:T(8,128)(2,1)}, bf16[192,2048]{1,0:T(8,128)(2,1)}) custom-call(bf16[32,768]{1,0:T(8,128)(2,1)} %pad_maximum_fusion.h_ref, bf16[1,768]{1,0:T(2,128)(2,1)} %get-tuple-element.36.gain_ref, bf16[2,192,384]{2,1,0:T(8,128)(2,1)} %refs_9_.1, ...), custom_call_target="tpu_custom_call" | custom-call | flops 3000000000 | bytes 8388608 | tf_op jit(solution)/shard_map/start/pallas_call | solution.py:453
  29.5 0.6 collective-permute-start.1
  30.1 1.5 %collective-permute-start = (bf16[2,192,1152]{2,1,0:T(8,128)(2,1)}, bf16[2,192,1152]{2,1,0:T(8,128)(2,1)}, u32[]{:S(2)}, u32[]{:S(2)}) collective-permute-start(bf16[2,192,1152]{2,1,0:T(8,128)(2,1)} %get-tuple-element.20.refs_3_), channel_id=1, source_target_pairs={{0,4},{4,0},{1,5},{5,1},{2,6},{6,2},{3,7},{7,3}} | collective-permute-start | bytes 2654216 | tf_op jit(solution)/shard_map/ppermute | solution.py:518
  31.6 1.6 %fusion.tab_ref = f32[16,512]{1,0:T(8,128)} fusion(f32[32,512]{1,0:T(8,128)} %constant.5.clone, f32[32,12]{0,1:T(8,128)} %param.26), kind=kOutput, calls=%fused_computation.1 | convolution fusion | flops 3145728 | bytes 99840 | tf_op jit(solution)/shard_map/dot_general | solution.py:471
  33.2 19.1 %self_attn.2 = (bf16[2,16,768,512]{3,2,1,0:T(8,128)(2,1)}, bf16[2,16,768,512]{3,2,1,0:T(8,128)(2,1)}, f32[2,16,768]{2,1,0:T(8,128)}) custom-call(s32[16]{0:T(128)} %pos_ref.3, f32[2,32,1152]{2,1,0:T(8,128)} %get-tuple-element.17.qkv_ref, f32[16,512]{1,0:T(8,128)} %fusion.tab_ref, bf16[2,16,768,512]{3,2,1,0:T(8,128)(2,1)} %bitcast.22, ...), custom_call_target="tpu_custom_call" | custom-call | flops 20000000000 | bytes 50331648 | tf_op jit(solution)/shard_map/self_attn/pallas_call | solution.py:144
  52.3 1.4 %fusion.3 = (bf16[1,768]{1,0:T(2,128)(2,1)}, bf16[1,768]{1,0:T(2,128)(2,1)}, bf16[1,768]{1,0:T(2,128)(2,1)}, bf16[1,768]{1,0:T(2,128)(2,1)}) fusion(bf16[2,768]{1,0:T(2,128)(2,1)} %param.29, bf16[2,768]{1,0:T(2,128)(2,1)} %param.28), kind=kLoop, calls=%fused_computation.4 | loop fusion | bytes 12288 | tf_op jit(solution)/shard_map/slice | solution.py:504
  53.6 0.0 collective-permute-done.1.refs_5_
  53.6 0.0 collective-permute-done.refs_4_
  53.6 35.5 %layer.1 = (f32[32,768]{1,0:T(8,128)}, f32[2,32,1152]{2,1,0:T(8,128)}, bf16[2,192,1152]{2,1,0:T(8,128)(2,1)}, bf16[192,2048]{1,0:T(8,128)(2,1)}) custom-call(s32[16]{0:T(128)} %len_ref.3, f32[32,768]{1,0:T(8,128)} %bitcast.34, f32[32,768]{1,0:T(8,128)} %get-tuple-element.19.x_ref, bf16[1,768]{1,0:T(2,128)(2,1)} %get-tuple-element.37.gcross_ref, ...), custom_call_target="tpu_custom_call" | custom-call | flops 20000000000 | bytes 8388608 | tf_op jit(solution)/shard_map/layer/pallas_call | solution.py:453
  89.2 1.1 collective-permute-start.3
  90.3 1.0 collective-permute-start.2
  91.2 19.0 %self_attn.3 = (bf16[2,16,768,512]{3,2,1,0:T(8,128)(2,1)}, bf16[2,16,768,512]{3,2,1,0:T(8,128)(2,1)}, f32[2,16,768]{2,1,0:T(8,128)}) custom-call(s32[16]{0:T(128)} %pos_ref.3, f32[2,32,1152]{2,1,0:T(8,128)} %get-tuple-element.22.qkv_ref, f32[16,512]{1,0:T(8,128)} %fusion.tab_ref, ...), custom_call_target="tpu_custom_call", output_to_operand_aliasing={{0}: (5, {}), {1}: (6, {})} | custom-call | flops 20000000000 | bytes 50331648 | tf_op jit(solution)/shard_map/self_attn/pallas_call | solution.py:144
  110.3 0.0 collective-permute-done.3.refs_4_
  110.3 0.0 collective-permute-done.2.refs_3_
  110.3 25.9 %last.1 = bf16[32,768]{1,0:T(8,128)(2,1)} custom-call(s32[16]{0:T(128)} %len_ref.3, f32[32,768]{1,0:T(8,128)} %bitcast.33, f32[32,768]{1,0:T(8,128)} %get-tuple-element.26.x_ref, bf16[1,768]{1,0:T(2,128)(2,1)} %get-tuple-element.38.gcross_ref, bf16[1,768]{1,0:T(2,128)(2,1)} %get-tuple-element.31.gmlp_ref, bf16[2,16,768,512]{3,2,1,0:T(8,128)(2,1)} %bitcast.30, ...), custom_call_target="tpu_custom_call" | custom-call | flops 20000000000 | bytes 8388608 | tf_op jit(solution)/shard_map/last/pallas_call | solution.py:453
  136.2 1.4 %copy.30 = bf16[2,16,768]{2,1,0:T(8,128)(2,1)} copy(bf16[2,16,768]{2,1,0:T(8,128)(2,1)} %bitcast.28) | data formatting | bytes 98304
Async XLA Ops:
  29.5 24.1 %collective-permute-start.1 = (bf16[192,2048]{1,0:T(8,128)(2,1)}, bf16[192,2048]{1,0:T(8,128)(2,1)}, u32[]{:S(2)}, u32[]{:S(2)}) collective-permute-start(bf16[192,2048]{1,0:T(8,128)(2,1)} %get-tuple-element.21), channel_id=1, source_target_pairs={{0,2},{1,3},{2,0},{3,1},{4,6},{5,7},{6,4},{7,5}} | collective-permute-start | bytes 2359304 | tf_op jit(solution)/shard_map/ppermute | solution.py:519
  30.1 23.6 %collective-permute-start = (bf16[2,192,1152]{2,1,0:T(8,128)(2,1)}, bf16[2,192,1152]{2,1,0:T(8,128)(2,1)}, u32[]{:S(2)}, u32[]{:S(2)}) collective-permute-start(bf16[2,192,1152]{2,1,0:T(8,128)(2,1)} %get-tuple-element.20.refs_3_), channel_id=1, source_target_pairs={{0,4},{4,0},{1,5},{5,1},{2,6},{6,2},{3,7},{7,3}} | collective-permute-start | bytes 2654216 | tf_op jit(solution)/shard_map/ppermute | solution.py:518
  89.2 21.1 %collective-permute-start.3 = (bf16[192,2048]{1,0:T(8,128)(2,1)}, bf16[192,2048]{1,0:T(8,128)(2,1)}, u32[]{:S(2)}, u32[]{:S(2)}) collective-permute-start(bf16[192,2048]{1,0:T(8,128)(2,1)} %get-tuple-element.28), channel_id=1, source_target_pairs={{0,2},{1,3},{2,0},{3,1},{4,6},{5,7},{6,4},{7,5}} | collective-permute-start | bytes 2359304 | tf_op jit(solution)/shard_map/ppermute | solution.py:519
  90.3 20.0 %collective-permute-start.2 = (bf16[2,192,1152]{2,1,0:T(8,128)(2,1)}, bf16[2,192,1152]{2,1,0:T(8,128)(2,1)}, u32[]{:S(2)}, u32[]{:S(2)}) collective-permute-start(bf16[2,192,1152]{2,1,0:T(8,128)(2,1)} %get-tuple-element.27.refs_2_), channel_id=1, source_target_pairs={{0,4},{4,0},{1,5},{5,1},{2,6},{6,2},{3,7},{7,3}} | collective-permute-start | bytes 2654216 | tf_op jit(solution)/shard_map/ppermute | solution.py:518

commit v2 on v1

--- a/solution.py
+++ b/solution.py
@@ -2,7 +2,6 @@
 
 import jax
 import jax.numpy as jnp
-import numpy as np
 from jax import lax
 from jax.experimental import pallas as pl
 from jax.experimental.pallas import tpu as pltpu
@@ -294,23 +293,31 @@
 
 class Whole:
     def __init__(self, st, packs, dst, sems):
-        block = packs[0].shape[1]
+        block, half = packs[0].shape[1], D // 2
         self.locals, self.shares = [], []
-        for n, (pack, cb) in enumerate(zip(packs, (st.c, 1 - st.c))):
-            for m, owner in enumerate((st.r, st.across)):
-                place = dst.at[cb, pl.ds(pl.multiple_of(owner * block, block), block), :]
-                self.locals.append(pltpu.make_async_copy(pack.at[m], place, sems.at[n, m, 0]))
-                self.shares.append(st.remote(pack.at[m], place, sems.at[n, m, 1], sems.at[n, m, 2], st.partner))
+        for w in range(packs[0].shape[2] // half):
+            cols = pl.ds(w * half, half)
+            self.locals.append([])
+            self.shares.append([])
+            for n, (pack, cb) in enumerate(zip(packs, (st.c, 1 - st.c))):
+                for m, owner in enumerate((st.r, st.across)):
+                    src = pack.at[m, :, cols]
+                    place = dst.at[cb, pl.ds(pl.multiple_of(owner * block, block), block), cols]
+                    sem = sems.at[w, n, m]
+                    self.locals[w].append(pltpu.make_async_copy(src, place, sem.at[0]))
+                    self.shares[w].append(st.remote(src, place, sem.at[1], sem.at[2], st.partner))
 
     def open_local(self):
-        each(self.locals, "start")
+        for copies in self.locals:
+            each(copies, "start")
 
     def open_share(self):
-        each(self.shares, "start")
-
-    def finish(self):
-        each(self.locals, "wait")
-        each(self.shares, "wait")
+        for copies in self.shares:
+            each(copies, "start")
+
+    def finish(self, w):
+        each(self.locals[w], "wait")
+        each(self.shares[w], "wait")
 
 
 class NextLayer:
@@ -329,8 +336,25 @@
         each(self.sends, "wait")
 
 
-def start_kernel(h_ref, gain_ref, wq_r, wk_r, wv_r, wo_r, wc_r, wco_r, wg_r, wu_r,
-                 x_ref, qkv_ref, pack_ref, tail_ref, hbuf, wqkv, qbuf, pbuf, tbuf, wsem, nsem, xsem, sem):
+def bias_table(bias_ref, tab_ref):
+    buckets, length = bias_ref.shape[1], tab_ref.shape[1]
+    dist = length - 1 - lax.broadcasted_iota(jnp.int32, (buckets, length), 1)
+    far = jnp.full((buckets, length), BUCKET_EDGES[0] - 1, jnp.int32)
+    for edge in BUCKET_EDGES:
+        far = far + jnp.where(dist >= edge, 1, 0)
+    bucket = jnp.where(dist < BUCKET_EDGES[0], dist, far)
+    pick = jnp.where(bucket == lax.broadcasted_iota(jnp.int32, (buckets, length), 0), 1.0, 0.0).astype(BF16)
+    left = jnp.concatenate([bias_ref[...], jnp.zeros((HROWS - bias_ref.shape[0], buckets), F32)], axis=0)
+    total = jnp.zeros((HROWS, length), F32)
+    for _ in range(3):
+        part = left.astype(BF16)
+        total = total + dot32(part, pick)
+        left = left - part.astype(F32)
+    tab_ref[...] = total
+
+
+def start_kernel(first_ref, second_ref, gain_ref, bias_ref, wq_r, wk_r, wv_r, wo_r, wc_r, wco_r, wg_r, wu_r,
+                 x_ref, qkv_ref, pack_ref, tail_ref, tab_ref, hbuf, wqkv, qbuf, pbuf, tbuf, wsem, nsem, xsem, sem):
     st = Stage()
     weights = weights_of(st, (wq_r, wk_r, wv_r), 0, wqkv, wsem)
     coming = NextLayer(st, (wo_r, wc_r, wco_r), (wg_r, wu_r), 0, pack_ref, tail_ref, pbuf, tbuf, nsem, xsem)
@@ -340,9 +364,11 @@
     each(weights, "open_cross")
     each(coming.sends, "start")
     each(weights, "open_share")
-    res = st.trade_rows(h_ref[...], hbuf, sem.at[0]).astype(F32)
-    x_ref[...] = res[:h_ref.shape[0]]
-    normed = rms(res, gain_ref[...])
+    hidden = jnp.concatenate([first_ref[...], second_ref[...]], axis=0)
+    x_ref[...] = hidden.astype(F32)
+    res = st.trade_rows(hidden, hbuf, sem.at[0]).astype(F32)
+    normed = rms(res, gain_ref[0:1, :])
+    bias_table(bias_ref, tab_ref)
     coming.store()
     each(weights, "relay")
     each(weights, "finish")
@@ -359,7 +385,7 @@
 def layer_kernel(layer, last, seqs, len_ref, o_ref, x_ref, gcross_ref, gmlp_ref, *refs):
     if last:
         (ck, cv, pack_in, ypack_in, xtail_in, wg_r, wu_r, wd_r, hid_ref,
-         kbuf, vbuf, wattn, wtail, wdown, qs, os, ubuf, kvsem, asem, wtsem, dsem, sem, sem2, nbuf, zbuf, zs) = refs
+         kbuf, vbuf, wattn, wtail, wdown, qs, os, ubuf, kvsem, asem, wtsem, dsem, sem, sem2, rbuf, zbuf, zs) = refs
     else:
         (gself_ref, ck, cv, pack_in, ypack_in, xtail_in, wg_r, wu_r, wd_r, wq_r, wk_r, wv_r, wo_r, wc_r, wco_r,
          x_out, qkv_ref, pack_ref, tail_ref,
@@ -394,10 +420,11 @@
         each(coming.sends, "start")
         each(ahead, "open_local")
         each(coming.loads, "start")
-    attn.finish()
+    attn.finish(0)
     y = jnp.concatenate(both_blocks(o_ref[...].astype(BF16), wattn, 0), axis=1)
     res = x_ref[...] + y.astype(F32)
-    for cb, q in enumerate(both_blocks(rms(res, gcross_ref[...]), wattn, 1)):
+    attn.finish(1)
+    for cb, q in enumerate(both_blocks(rms(res, gcross_ref[layer:layer + 1, :]), wattn, 1)):
         qs[cb] = q.astype(F32)
     each(tail, "open_share")
     each(down, "open_share")
@@ -419,29 +446,42 @@
 
     lax.fori_loop(0, seqs // SEQ_BLOCK, cross_step, 0)
     each(down, "relay")
+    attn.finish(2)
     y = jnp.concatenate(both_blocks(os[...].reshape(rows, D).astype(BF16), wattn, 2), axis=1)
     res = res + y.astype(F32)
-    if last:
-        normed = st.trade_rows(rms(res, gmlp_ref[...]), nbuf, sem.at[0])
-    else:
-        res = st.trade_rows(res, rbuf, sem.at[0])
-        normed = rms(res, gmlp_ref[...])
+    gain = gmlp_ref[layer:layer + 1, :]
+    ff = wtail.shape[1] // 2
+
+    def gated(normed):
+        gate = dot32(normed, wtail[:, 0:ff]).astype(BF16).astype(F32)
+        up = dot32(normed, wtail[:, ff:2 * ff]).astype(BF16).astype(F32)
+        return (gate * jax.nn.sigmoid(gate) * up).astype(BF16)
+
+    normed = rms(res, gain)
+    rbuf[0] = normed if last else res
+    moving = st.send(rbuf.at[0], rbuf.at[1], sem.at[0])
     each(tail, "finish")
-    ff = wtail.shape[1] // 2
-    gate = dot32(normed, wtail[:, 0:ff]).astype(BF16).astype(F32)
-    up = dot32(normed, wtail[:, ff:2 * ff]).astype(BF16).astype(F32)
-    act = st.trade_columns(gate * jax.nn.sigmoid(gate) * up, ubuf, sem2.at[0])
+    ubuf[st.c, 0] = gated(normed)
+    moving_own = st.send(ubuf.at[st.c, 0], ubuf.at[st.c, 1], sem2.at[0, 0])
+    moving.wait()
+    ubuf[st.c, 1] = gated(rbuf[1] if last else rms(rbuf[1], gain))
+    moving_other = st.send(ubuf.at[st.c, 1], ubuf.at[st.c, 0], sem2.at[0, 1])
+    if not last:
+        res = jnp.concatenate([res, rbuf[1]], axis=0)
+    moving_own.wait()
+    moving_other.wait()
+    act = jnp.concatenate([ubuf[0].reshape(2 * rows, ff), ubuf[1].reshape(2 * rows, ff)], axis=1)
     if not last:
         each(ahead, "relay")
     each(down, "finish")
     z = dot32(act, wdown[...])
     if last:
         st.give_rows(z, zbuf, sem.at[1], zs)
-        hid_ref[...] = (res + jnp.concatenate([zs[0], zs[1]], axis=1)).astype(BF16)
+        hid_ref[...] = res + jnp.concatenate([zs[0], zs[1]], axis=1)
     else:
         res = res + st.trade_columns(z, zbuf, sem2.at[1]).astype(F32)
         x_out[...] = res[:rows]
-        normed = rms(res, gself_ref[...])
+        normed = rms(res, gself_ref[layer + 1:layer + 2, :])
         each(ahead, "finish")
         st.give_rows(dot32(normed, wqkv[...]), qkvbuf, sem.at[1], qkv_ref)
         coming.finish()
@@ -462,16 +502,6 @@
     )(*args)
 
 
-def bias_table(dec_bias, cache_len):
-    dist = np.arange(cache_len)[::-1]
-    far = BUCKET_EDGES[0] - 1 + np.sum(dist[:, None] >= np.array(BUCKET_EDGES)[None, :], axis=1)
-    bucket = np.where(dist < BUCKET_EDGES[0], dist, far)
-    onehot = (np.arange(dec_bias.shape[0])[:, None] == bucket[None, :]).astype(np.float32)
-    padded = jnp.pad(dec_bias, ((0, 0), (0, HROWS - dec_bias.shape[1])))
-    return lax.dot_general(padded, jnp.asarray(onehot), (((0,), (0,)), ((), ())),
-                           precision=lax.Precision.HIGHEST, preferred_element_type=F32)
-
-
 def solution(mesh):
     batch_axes = ('dp', 'col', 'row')
 
@@ -489,7 +519,6 @@
             return jnp.transpose(cache, (0, 1, 3, 4, 2)).reshape(layers, seqs, D, cache.shape[2])
 
         caches = [flat(a) for a in (self_k, self_v, cross_k, cross_v)]
-        table = bias_table(dec_bias, cache_len)
         block = w_query.shape[1]
 
         vm = lambda shape, dt=BF16: pltpu.VMEM(shape, dt)
@@ -501,15 +530,14 @@
         pack_t = ("h", jax.ShapeDtypeStruct((2, block, 3 * half), BF16))
         tail_t = ("h", jax.ShapeDtypeStruct((block, 2 * ffc), BF16))
         coming = [vm((block, 3 * half)), vm((block, 2 * ffc))]
-        gain = lambda g, l: g[l][None, :]
         across = [(r, (r + 2) % 4) for r in range(4)]
         flip = [(0, 1), (1, 0)]
 
-        hidden = jnp.concatenate([h_first, h_second], axis=0)
-        res, qkv, pack, tail_own = exchange_call(
-            start_kernel, 0, "start", "vv" + "h" * 8,
-            [hidden, gain(norm_self, 0), w_query, w_key, w_value, w_out, w_cquery, w_cout, w_gate, w_up],
-            [res_t, qkv_t, pack_t, tail_t],
+        table_t = ("v", jax.ShapeDtypeStruct((HROWS, cache_len), F32))
+        res, qkv, pack, tail_own, table = exchange_call(
+            start_kernel, 0, "start", "vvvv" + "h" * 8,
+            [h_first, h_second, norm_self, dec_bias.T, w_query, w_key, w_value, w_out, w_cquery, w_cout, w_gate, w_up],
+            [res_t, qkv_t, pack_t, tail_t, table_t],
             [rowbuf(D), vm((depth, 3 * half)), rowbuf(3 * half)] + coming
             + [dma(3, 7), dma(3, 3), dma(3, 2), dma(2, 2)], 3_000_000_000)
         outs = None
@@ -522,27 +550,27 @@
             cache_buf = vm((seqs, D, cross_k.shape[2]))
             scratch = [cache_buf, cache_buf, vm((2, depth, 3 * half)), vm((depth, 2 * ffc)), vm((fdepth, half)),
                        vm((2, rows, half), F32), vm((TOKENS, seqs, D), F32), colbuf(ffc),
-                       dma(2, seqs), dma(2, 2, 3), dma(2, 7), dma(1, 7), dma(2, 2), dma(2, 2, 2)]
-            args = [enc_lens, mixed.reshape(rows, D), res, gain(norm_cross, l), gain(norm_mlp, l)]
+                       dma(2, seqs), dma(3, 2, 2, 3), dma(2, 7), dma(1, 7), dma(2, 2), dma(2, 2, 2)]
+            args = [enc_lens, mixed.reshape(rows, D), res, norm_cross, norm_mlp]
             weights = [caches[2], caches[3], pack, ypack, xtail, w_gate, w_up, w_down]
             if last:
                 hid, = exchange_call(
                     functools.partial(layer_kernel, l, True, seqs), 1 + l, "last", "svvvv" + "h" * 8,
-                    args + weights, [("v", jax.ShapeDtypeStruct((rows, D), BF16))],
+                    args + weights, [res_t],
                     scratch + [rowbuf(D), rowbuf(half), vm((2, rows, half), F32)], 20_000_000_000)
             else:
                 scratch += [rowbuf(D, F32), colbuf(half), vm((depth, 3 * half)), rowbuf(3 * half)] + coming
                 scratch += [dma(3, 7), dma(3, 3), dma(3, 2)]
                 res, qkv, pack, tail_own = exchange_call(
                     functools.partial(layer_kernel, l, False, seqs), 1 + l, "layer", "svvvvv" + "h" * 14,
-                    args + [gain(norm_self, l + 1)] + weights
+                    args + [norm_self] + weights
                     + [w_query, w_key, w_value, w_out, w_cquery, w_cout],
                     [res_t, qkv_t, pack_t, tail_t], scratch, 20_000_000_000)
 
         def unflat(cache):
             return jnp.transpose(cache.reshape(layers, seqs, HEADS, HEAD_DIM, cache_len), (0, 1, 4, 2, 3))
 
-        return hid.reshape(TOKENS, seqs, D), unflat(outs[0]), unflat(outs[1])
+        return hid.reshape(TOKENS, seqs, D).astype(BF16), unflat(outs[0]), unflat(outs[1])
 
     row_spec = P(batch_axes, None)
     seq_spec = P(batch_axes)

time: 138 us -> 132 us (0.957)
  local copies, waits for them, and re-layouts: 4.16 us -> 0 us
  matrix products: 1.64 us -> 0 us
    slice x2 -> x0, local copies, waits for them, and re-layouts: 2.74 us -> none  [local_step(): gain = lambda g, l: g[l][None, :]]
    dot_general x1 -> x0, matrix products: 1.64 us -> none  [bias_table(): lax.dot_general(padded, jnp.asarray(onehot), (((0,), (0,)), ((), ())), pr...]
    convert_element_type x0 -> x1, other arithmetic: none -> 1.52 us  [local_step(): hid.reshape(TOKENS, seqs, D).astype(BF16)]
    unnamed x1 -> x0, local copies, waits for them, and re-layouts: 1.42 us -> none
  transfers between devices with their start and end apart: 4 -> 4, of which waited for: 0 -> 0; matrix products, arithmetic and copies ran while one was open for 2% -> 0% of each run, Pallas kernels for 28% -> 29%
where the time goes in v2:
time: 132 us
  Pallas kernels  125 us (95%)
  starting transfers between devices  4.71 us (4%)
  other arithmetic  1.52 us (1%)
    pallas_call x3, Pallas kernels, exchange_call(): pl.pallas_call(kernel, out_shape=tuple((t for _, t in outs)), in_specs=sp...  86.6 us
    pallas_call x2, Pallas kernels, self_attention(): pl.pallas_call(functools.partial(self_kernel, layer, seqs, outs is not No...  38.1 us
    ppermute x2, starting transfers between devices, local_step(): ypack = lax.ppermute(pack, 'col', flip)  2.89 us
  transfers between devices with their start and end apart: 4, of which 0 were waited for; matrix products, arithmetic and copies ran while one was open for 0% of the time, Pallas kernels for 29%

profile of v2, /device:TPU:0, one launch (start us, length us, event | category | flops | bytes accessed | tf_op | source)
XLA Modules:
  0.0 131.7 jit_solution(13796658174953105928)
XLA Ops:
  0.6 26.1 %start.1 = (f32[32,768]{1,0:T(8,128)}, f32[2,32,1152]{2,1,0:T(8,128)}, bf16[2,192,1152]{2,1,0:T(8,128)(2,1)}, bf16[192,2048]{1,0:T(8,128)(2,1)}, f32[16,512]{1,0:T(8,128)}) custom-call(bf16[16,768]{1,0:T(8,128)(2,1)} %first_ref.1, bf16[16,768]{1,0:T(8,128)(2,1)} %second_ref.1, bf16[2,768]{1,0:T(2,128)(2,1)} %refs_0_.1, f32[12,32]{1,0:T(8,128)} %bitcast.34, ...), custom_call_target="tpu_custom_call" | custom-call | flops 3000000000 | bytes 8388608 | tf_op jit(solution)/shard_map/start/pallas_call | solution.py:493
  26.8 0.6 collective-permute-start.1
  27.3 1.5 %collective-permute-start = (bf16[2,192,1152]{2,1,0:T(8,128)(2,1)}, bf16[2,192,1152]{2,1,0:T(8,128)(2,1)}, u32[]{:S(2)}, u32[]{:S(2)}) collective-permute-start(bf16[2,192,1152]{2,1,0:T(8,128)(2,1)} %get-tuple-element.22.refs_3_), channel_id=1, source_target_pairs={{0,4},{4,0},{1,5},{5,1},{2,6},{6,2},{3,7},{7,3}} | collective-permute-start | bytes 2654216 | tf_op jit(solution)/shard_map/ppermute | solution.py:546
  28.8 19.1 %self_attn.2 = (bf16[2,16,768,512]{3,2,1,0:T(8,128)(2,1)}, bf16[2,16,768,512]{3,2,1,0:T(8,128)(2,1)}, f32[2,16,768]{2,1,0:T(8,128)}) custom-call(s32[16]{0:T(128)} %pos_ref.3, f32[2,32,1152]{2,1,0:T(8,128)} %get-tuple-element.18.qkv_ref, f32[16,512]{1,0:T(8,128)} %get-tuple-element.19.tab_ref, bf16[2,16,768,512]{3,2,1,0:T(8,128)(2,1)} %bitcast.22, ...), custom_call_target="tpu_custom_call" | custom-call | flops 20000000000 | bytes 50331648 | tf_op jit(solution)/shard_map/self_attn/pallas_call | solution.py:143
  47.9 0.0 collective-permute-done.1.refs_5_
  47.9 0.0 collective-permute-done.refs_4_
  47.9 35.6 %layer.1 = (f32[32,768]{1,0:T(8,128)}, f32[2,32,1152]{2,1,0:T(8,128)}, bf16[2,192,1152]{2,1,0:T(8,128)(2,1)}, bf16[192,2048]{1,0:T(8,128)(2,1)}) custom-call(s32[16]{0:T(128)} %len_ref.3, f32[32,768]{1,0:T(8,128)} %bitcast.35, f32[32,768]{1,0:T(8,128)} %get-tuple-element.21.x_ref, bf16[2,768]{1,0:T(2,128)(2,1)} %gcross_ref.3, bf16[2,768]{1,0:T(2,128)(2,1)} %gmlp_ref.3, ...), custom_call_target="tpu_custom_call" | custom-call | flops 20000000000 | bytes 8388608 | tf_op jit(solution)/shard_map/layer/pallas_call | solution.py:493
  83.5 1.3 collective-permute-start.3
  84.8 1.4 %collective-permute-start.2 = (bf16[2,192,1152]{2,1,0:T(8,128)(2,1)}, bf16[2,192,1152]{2,1,0:T(8,128)(2,1)}, u32[]{:S(2)}, u32[]{:S(2)}) collective-permute-start(bf16[2,192,1152]{2,1,0:T(8,128)(2,1)} %get-tuple-element.29.refs_2_), channel_id=1, source_target_pairs={{0,4},{4,0},{1,5},{5,1},{2,6},{6,2},{3,7},{7,3}} | collective-permute-start | bytes 2654216 | tf_op jit(solution)/shard_map/ppermute | solution.py:546
  86.2 19.1 %self_attn.3 = (bf16[2,16,768,512]{3,2,1,0:T(8,128)(2,1)}, bf16[2,16,768,512]{3,2,1,0:T(8,128)(2,1)}, f32[2,16,768]{2,1,0:T(8,128)}) custom-call(s32[16]{0:T(128)} %pos_ref.3, f32[2,32,1152]{2,1,0:T(8,128)} %get-tuple-element.24.qkv_ref, f32[16,512]{1,0:T(8,128)} %get-tuple-element.19.tab_ref, ...), custom_call_target="tpu_custom_call", output_to_operand_aliasing={{0}: (5, {}), {1}: (6, {})} | custom-call | flops 20000000000 | bytes 50331648 | tf_op jit(solution)/shard_map/self_attn/pallas_call | solution.py:143
  105.3 0.0 collective-permute-done.3.refs_4_
  105.3 0.0 collective-permute-done.2.refs_3_
  105.3 24.8 %last.1 = f32[32,768]{1,0:T(8,128)} custom-call(s32[16]{0:T(128)} %len_ref.3, f32[32,768]{1,0:T(8,128)} %bitcast.33, f32[32,768]{1,0:T(8,128)} %get-tuple-element.28.x_ref, bf16[2,768]{1,0:T(2,128)(2,1)} %gcross_ref.3, bf16[2,768]{1,0:T(2,128)(2,1)} %gmlp_ref.3, bf16[2,16,768,512]{3,2,1,0:T(8,128)(2,1)} %bitcast.30, bf16[2,16,768,512]{3,2,1,0:T(8,128)(2,1)} %bitcast.32, ...), custom_call_target="tpu_custom_call" | custom-call | flops 20000000000 | bytes 8388608 | tf_op jit(solution)/shard_map/last/pallas_call | solution.py:493
  130.1 1.5 %convert_element_type.6 = bf16[32,768]{1,0:T(8,128)(2,1)} convert(f32[32,768]{1,0:T(8,128)} %last.1) | non-fusion elementwise | flops 24576 | bytes 147456 | tf_op jit(solution)/shard_map/convert_element_type | solution.py:573
Async XLA Ops:
  26.8 21.1 %collective-permute-start.1 = (bf16[192,2048]{1,0:T(8,128)(2,1)}, bf16[192,2048]{1,0:T(8,128)(2,1)}, u32[]{:S(2)}, u32[]{:S(2)}) collective-permute-start(bf16[192,2048]{1,0:T(8,128)(2,1)} %get-tuple-element.23), channel_id=1, source_target_pairs={{0,2},{1,3},{2,0},{3,1},{4,6},{5,7},{6,4},{7,5}} | collective-permute-start | bytes 2359304 | tf_op jit(solution)/shard_map/ppermute | solution.py:547
  27.3 20.6 %collective-permute-start = (bf16[2,192,1152]{2,1,0:T(8,128)(2,1)}, bf16[2,192,1152]{2,1,0:T(8,128)(2,1)}, u32[]{:S(2)}, u32[]{:S(2)}) collective-permute-start(bf16[2,192,1152]{2,1,0:T(8,128)(2,1)} %get-tuple-element.22.refs_3_), channel_id=1, source_target_pairs={{0,4},{4,0},{1,5},{5,1},{2,6},{6,2},{3,7},{7,3}} | collective-permute-start | bytes 2654216 | tf_op jit(solution)/shard_map/ppermute | solution.py:546
  83.5 21.7 %collective-permute-start.3 = (bf16[192,2048]{1,0:T(8,128)(2,1)}, bf16[192,2048]{1,0:T(8,128)(2,1)}, u32[]{:S(2)}, u32[]{:S(2)}) collective-permute-start(bf16[192,2048]{1,0:T(8,128)(2,1)} %get-tuple-element.30), channel_id=1, source_target_pairs={{0,2},{1,3},{2,0},{3,1},{4,6},{5,7},{6,4},{7,5}} | collective-permute-start | bytes 2359304 | tf_op jit(solution)/shard_map/ppermute | solution.py:547
  84.8 20.5 %collective-permute-start.2 = (bf16[2,192,1152]{2,1,0:T(8,128)(2,1)}, bf16[2,192,1152]{2,1,0:T(8,128)(2,1)}, u32[]{:S(2)}, u32[]{:S(2)}) collective-permute-start(bf16[2,192,1152]{2,1,0:T(8,128)(2,1)} %get-tuple-element.29.refs_2_), channel_id=1, source_target_pairs={{0,4},{4,0},{1,5},{5,1},{2,6},{6,2},{3,7},{7,3}} | collective-permute-start | bytes 2654216 | tf_op jit(solution)/shard_map/ppermute | solution.py:546

commit v3 on v2

--- a/solution.py
+++ b/solution.py
@@ -291,48 +291,39 @@
     return copies
 
 
-class Whole:
-    def __init__(self, st, packs, dst, sems):
-        block, half = packs[0].shape[1], D // 2
-        self.locals, self.shares = [], []
-        for w in range(packs[0].shape[2] // half):
-            cols = pl.ds(w * half, half)
-            self.locals.append([])
-            self.shares.append([])
-            for n, (pack, cb) in enumerate(zip(packs, (st.c, 1 - st.c))):
-                for m, owner in enumerate((st.r, st.across)):
-                    src = pack.at[m, :, cols]
-                    place = dst.at[cb, pl.ds(pl.multiple_of(owner * block, block), block), cols]
-                    sem = sems.at[w, n, m]
-                    self.locals[w].append(pltpu.make_async_copy(src, place, sem.at[0]))
-                    self.shares[w].append(st.remote(src, place, sem.at[1], sem.at[2], st.partner))
-
-    def open_local(self):
-        for copies in self.locals:
-            each(copies, "start")
-
-    def open_share(self):
-        for copies in self.shares:
-            each(copies, "start")
-
-    def finish(self, w):
-        each(self.locals[w], "wait")
-        each(self.shares[w], "wait")
+class Second:
+    def __init__(self, st, own, crossed, dst, sems):
+        depth = own.shape[0]
+        self.sends, self.relays = [], []
+        for n, (src, owner) in enumerate(((own, st.r), (crossed, st.across))):
+            at = pl.ds(pl.multiple_of(owner * depth, depth), depth)
+            theirs, mine = dst.at[st.c, at, :], dst.at[1 - st.c, at, :]
+            self.sends.append(st.remote(src, theirs, sems.at[n, 0], sems.at[n, 1], st.peer))
+            self.relays.append(st.remote(mine, mine, sems.at[n, 2], sems.at[n, 3], st.partner))
+
+    def relay(self):
+        for send, relay in zip(self.sends, self.relays):
+            send.wait_recv()
+            relay.start()
+
+    def finish(self):
+        for send, relay in zip(self.sends, self.relays):
+            send.wait_send()
+            relay.wait()
 
 
 class NextLayer:
-    def __init__(self, st, attn, mlp, layer, pack_ref, tail_ref, pbuf, tbuf, sems, xsems):
-        self.loads = collect(attn, layer, pbuf, sems.at[0]) + collect(mlp, layer, tbuf, sems.at[1])
-        self.sends = forward(st, attn, layer, pack_ref.at[1], xsems)
-        self.stores = [pltpu.make_async_copy(pbuf, pack_ref.at[0], sems.at[2, 0]),
-                       pltpu.make_async_copy(tbuf, tail_ref, sems.at[2, 1])]
+    def __init__(self, st, mid, tail, layer, mid_ref, tail_ref, tbuf, sems, xsems):
+        self.loads = collect(tail, layer, tbuf, sems)
+        self.sends = forward(st, mid, layer, mid_ref, xsems)
+        self.out = pltpu.make_async_copy(tbuf, tail_ref, sems.at[len(tail)])
 
     def store(self):
         each(self.loads, "wait")
-        each(self.stores, "start")
+        self.out.start()
 
     def finish(self):
-        each(self.stores, "wait")
+        self.out.wait()
         each(self.sends, "wait")
 
 
@@ -354,10 +345,10 @@
 
 
 def start_kernel(first_ref, second_ref, gain_ref, bias_ref, wq_r, wk_r, wv_r, wo_r, wc_r, wco_r, wg_r, wu_r,
-                 x_ref, qkv_ref, pack_ref, tail_ref, tab_ref, hbuf, wqkv, qbuf, pbuf, tbuf, wsem, nsem, xsem, sem):
+                 x_ref, qkv_ref, mid_ref, tail_ref, tab_ref, hbuf, wqkv, qbuf, tbuf, wsem, nsem, xsem, sem):
     st = Stage()
     weights = weights_of(st, (wq_r, wk_r, wv_r), 0, wqkv, wsem)
-    coming = NextLayer(st, (wo_r, wc_r, wco_r), (wg_r, wu_r), 0, pack_ref, tail_ref, pbuf, tbuf, nsem, xsem)
+    coming = NextLayer(st, (wo_r, wc_r), (wco_r, wg_r, wu_r), 0, mid_ref, tail_ref, tbuf, nsem, xsem)
     each(weights, "open_local")
     each(coming.loads, "start")
     st.greet()
@@ -365,8 +356,8 @@
     each(coming.sends, "start")
     each(weights, "open_share")
     hidden = jnp.concatenate([first_ref[...], second_ref[...]], axis=0)
-    x_ref[...] = hidden.astype(F32)
     res = st.trade_rows(hidden, hbuf, sem.at[0]).astype(F32)
+    x_ref[...] = res
     normed = rms(res, gain_ref[0:1, :])
     bias_table(bias_ref, tab_ref)
     coming.store()
@@ -376,27 +367,29 @@
     coming.finish()
 
 
-def both_blocks(act, packed, which):
-    half = D // 2
-    cols = slice(which * half, (which + 1) * half)
-    return [dot32(act, packed[cb, :, cols]).astype(BF16) for cb in range(2)]
-
-
 def layer_kernel(layer, last, seqs, len_ref, o_ref, x_ref, gcross_ref, gmlp_ref, *refs):
+    if not last:
+        gself_ref, refs = refs[0], refs[1:]
+    ck, cv, mid_in, tail_in, wo_r, wc_r, wco_r, wg_r, wu_r, wd_r = refs[:10]
+    refs = refs[10:]
     if last:
-        (ck, cv, pack_in, ypack_in, xtail_in, wg_r, wu_r, wd_r, hid_ref,
-         kbuf, vbuf, wattn, wtail, wdown, qs, os, ubuf, kvsem, asem, wtsem, dsem, sem, sem2, rbuf, zbuf, zs) = refs
+        hid_ref, refs = refs[0], refs[1:]
     else:
-        (gself_ref, ck, cv, pack_in, ypack_in, xtail_in, wg_r, wu_r, wd_r, wq_r, wk_r, wv_r, wo_r, wc_r, wco_r,
-         x_out, qkv_ref, pack_ref, tail_ref,
-         kbuf, vbuf, wattn, wtail, wdown, qs, os, ubuf, kvsem, asem, wtsem, dsem, sem, sem2,
-         rbuf, zbuf, wqkv, qkvbuf, pbuf, tbuf, wsem, nsem, xsem) = refs
+        wq_r, wk_r, wv_r, x_out, qkv_ref, mid_ref, tail_ref = refs[:7]
+        refs = refs[7:]
+    (kbuf, vbuf, wmid, wco, wtail, wdown, qs, os, obuf, ybuf, qbuf, ubuf,
+     kvsem, msem, csem, c2sem, gsem, dsem, sem, sem2, rbuf, zbuf) = refs[:22]
+    refs = refs[22:]
     st = Stage()
-    rows = o_ref.shape[0]
-    attn = Whole(st, (pack_in, ypack_in), wattn, asem)
-    tail = weights_of(st, (wg_r, wu_r), layer, wtail, wtsem, xtail_in)
+    rows, half = o_ref.shape[0], D // 2
+    ff = wg_r.shape[2]
+    co_x, gate_x = tail_in.at[:, pl.ds(0, half)], tail_in.at[:, pl.ds(half, 2 * ff)]
+    mid = weights_of(st, (wo_r, wc_r), layer, wmid, msem, mid_in)
+    co = weights_of(st, (wco_r,), layer, wco.at[st.c], csem, co_x)
+    co_second = Second(st, wco_r.at[layer], co_x, wco, c2sem)
+    tail = weights_of(st, (wg_r, wu_r), layer, wtail, gsem, gate_x)
     down = weights_of(st, (wd_r,), layer, wdown, dsem)
-    attn.open_local()
+    each(mid, "open_local")
 
     def caches(b):
         return [pltpu.make_async_copy(src.at[layer, b], buf.at[b], kvsem.at[n, b])
@@ -406,26 +399,39 @@
         each(caches(b), "start")
         return carry
 
+    obuf[0] = o_ref[...].astype(BF16)
     st.greet()
-    attn.open_share()
+    moving = st.send(obuf.at[0], obuf.at[1], sem.at[2])
+    each(mid, "open_share")
+    co_second.sends[0].start()
     each(down, "open_cross")
     lax.fori_loop(0, seqs, fetch_caches, 0)
+    each(co, "open_local")
     each(tail, "open_local")
     each(down, "open_local")
     if not last:
+        wqkv, qkvbuf, tbuf, wsem, nsem, xsem = refs
         ahead = weights_of(st, (wq_r, wk_r, wv_r), layer + 1, wqkv, wsem)
-        coming = NextLayer(st, (wo_r, wc_r, wco_r), (wg_r, wu_r), layer + 1, pack_ref, tail_ref, pbuf, tbuf,
-                           nsem, xsem)
+        coming = NextLayer(st, (wo_r, wc_r), (wco_r, wg_r, wu_r), layer + 1, mid_ref, tail_ref, tbuf, nsem, xsem)
         each(ahead, "open_cross")
         each(coming.sends, "start")
         each(ahead, "open_local")
         each(coming.loads, "start")
-    attn.finish(0)
-    y = jnp.concatenate(both_blocks(o_ref[...].astype(BF16), wattn, 0), axis=1)
+    moving.wait()
+    each(mid, "finish")
+    mixed = jnp.concatenate([obuf[0], obuf[1]], axis=0)
+    y = dot32(mixed, wmid[:, 0:half]).astype(BF16)
+    ybuf[st.c] = y.reshape(2, rows, half)
+    moving = st.send(ybuf.at[st.c, 1], ybuf.at[st.c, 0], sem2.at[2, 0])
+    moving_own = st.send(ybuf.at[st.c, 0], ybuf.at[st.c, 1], sem2.at[2, 1])
+    co_second.sends[1].start()
+    each(co, "open_share")
+    moving.wait()
+    moving_own.wait()
+    y = jnp.concatenate([ybuf[0].reshape(2 * rows, half), ybuf[1].reshape(2 * rows, half)], axis=1)
     res = x_ref[...] + y.astype(F32)
-    attn.finish(1)
-    for cb, q in enumerate(both_blocks(rms(res, gcross_ref[layer:layer + 1, :]), wattn, 1)):
-        qs[cb] = q.astype(F32)
+    st.give_rows(dot32(rms(res, gcross_ref[layer:layer + 1, :]), wmid[:, half:D]), qbuf, sem.at[3], qs)
+    co_second.relay()
     each(tail, "open_share")
     each(down, "open_share")
     if not last:
@@ -446,28 +452,27 @@
 
     lax.fori_loop(0, seqs // SEQ_BLOCK, cross_step, 0)
     each(down, "relay")
-    attn.finish(2)
-    y = jnp.concatenate(both_blocks(os[...].reshape(rows, D).astype(BF16), wattn, 2), axis=1)
-    res = res + y.astype(F32)
+    each(co, "finish")
+    co_second.finish()
+    mixed = os[...].reshape(rows, D).astype(BF16)
+    y = jnp.concatenate([dot32(mixed, wco[0]), dot32(mixed, wco[1])], axis=1).astype(BF16)
+    rbuf[0] = y
+    moving = st.send(rbuf.at[0], rbuf.at[1], sem.at[0])
     gain = gmlp_ref[layer:layer + 1, :]
-    ff = wtail.shape[1] // 2
 
     def gated(normed):
         gate = dot32(normed, wtail[:, 0:ff]).astype(BF16).astype(F32)
         up = dot32(normed, wtail[:, ff:2 * ff]).astype(BF16).astype(F32)
         return (gate * jax.nn.sigmoid(gate) * up).astype(BF16)
 
-    normed = rms(res, gain)
-    rbuf[0] = normed if last else res
-    moving = st.send(rbuf.at[0], rbuf.at[1], sem.at[0])
+    res_own = res[:rows] + y.astype(F32)
     each(tail, "finish")
-    ubuf[st.c, 0] = gated(normed)
+    ubuf[st.c, 0] = gated(rms(res_own, gain))
     moving_own = st.send(ubuf.at[st.c, 0], ubuf.at[st.c, 1], sem2.at[0, 0])
     moving.wait()
-    ubuf[st.c, 1] = gated(rbuf[1] if last else rms(rbuf[1], gain))
+    res_other = res[rows:] + rbuf[1].astype(F32)
+    ubuf[st.c, 1] = gated(rms(res_other, gain))
     moving_other = st.send(ubuf.at[st.c, 1], ubuf.at[st.c, 0], sem2.at[0, 1])
-    if not last:
-        res = jnp.concatenate([res, rbuf[1]], axis=0)
     moving_own.wait()
     moving_other.wait()
     act = jnp.concatenate([ubuf[0].reshape(2 * rows, ff), ubuf[1].reshape(2 * rows, ff)], axis=1)
@@ -476,11 +481,12 @@
     each(down, "finish")
     z = dot32(act, wdown[...])
     if last:
+        zs, = refs
         st.give_rows(z, zbuf, sem.at[1], zs)
-        hid_ref[...] = res + jnp.concatenate([zs[0], zs[1]], axis=1)
+        hid_ref[...] = res_own + jnp.concatenate([zs[0], zs[1]], axis=1)
     else:
-        res = res + st.trade_columns(z, zbuf, sem2.at[1]).astype(F32)
-        x_out[...] = res[:rows]
+        res = jnp.concatenate([res_own, res_other], axis=0) + st.trade_columns(z, zbuf, sem2.at[1]).astype(F32)
+        x_out[...] = res
         normed = rms(res, gself_ref[layer + 1:layer + 2, :])
         each(ahead, "finish")
         st.give_rows(dot32(normed, wqkv[...]), qkvbuf, sem.at[1], qkv_ref)
@@ -525,47 +531,46 @@
         dma = lambda *shape: pltpu.SemaphoreType.DMA(shape)
         rowbuf = lambda width, dt=BF16: vm((2, rows, width), dt)
         colbuf = lambda width: vm((2, 2, rows, width))
-        res_t = ("v", jax.ShapeDtypeStruct((rows, D), F32))
+        res_t = ("v", jax.ShapeDtypeStruct((2 * rows, D), F32))
+        hid_t = ("v", jax.ShapeDtypeStruct((rows, D), F32))
         qkv_t = ("v", jax.ShapeDtypeStruct((2, rows, 3 * half), F32))
-        pack_t = ("h", jax.ShapeDtypeStruct((2, block, 3 * half), BF16))
-        tail_t = ("h", jax.ShapeDtypeStruct((block, 2 * ffc), BF16))
-        coming = [vm((block, 3 * half)), vm((block, 2 * ffc))]
+        mid_t = ("h", jax.ShapeDtypeStruct((block, D), BF16))
+        tail_t = ("h", jax.ShapeDtypeStruct((block, half + 2 * ffc), BF16))
+        coming = [vm((block, half + 2 * ffc))]
         across = [(r, (r + 2) % 4) for r in range(4)]
-        flip = [(0, 1), (1, 0)]
 
         table_t = ("v", jax.ShapeDtypeStruct((HROWS, cache_len), F32))
-        res, qkv, pack, tail_own, table = exchange_call(
+        res, qkv, mid, tail_own, table = exchange_call(
             start_kernel, 0, "start", "vvvv" + "h" * 8,
             [h_first, h_second, norm_self, dec_bias.T, w_query, w_key, w_value, w_out, w_cquery, w_cout, w_gate, w_up],
-            [res_t, qkv_t, pack_t, tail_t, table_t],
+            [res_t, qkv_t, mid_t, tail_t, table_t],
             [rowbuf(D), vm((depth, 3 * half)), rowbuf(3 * half)] + coming
-            + [dma(3, 7), dma(3, 3), dma(3, 2), dma(2, 2)], 3_000_000_000)
+            + [dma(3, 7), dma(4), dma(2, 2), dma(2, 2)], 3_000_000_000)
         outs = None
         for l in range(layers):
             last = l == layers - 1
-            ypack = lax.ppermute(pack, "col", flip)
             xtail = lax.ppermute(tail_own, "row", across)
             k_out, v_out, mixed = self_attention(l, start_pos, qkv, table, caches[0], caches[1], outs)
             outs = (k_out, v_out)
             cache_buf = vm((seqs, D, cross_k.shape[2]))
-            scratch = [cache_buf, cache_buf, vm((2, depth, 3 * half)), vm((depth, 2 * ffc)), vm((fdepth, half)),
-                       vm((2, rows, half), F32), vm((TOKENS, seqs, D), F32), colbuf(ffc),
-                       dma(2, seqs), dma(3, 2, 2, 3), dma(2, 7), dma(1, 7), dma(2, 2), dma(2, 2, 2)]
+            scratch = [cache_buf, cache_buf, vm((depth, D)), vm((2, depth, half)), vm((depth, 2 * ffc)),
+                       vm((fdepth, half)), vm((2, rows, half), F32), vm((TOKENS, seqs, D), F32),
+                       rowbuf(D), colbuf(half), rowbuf(half), colbuf(ffc),
+                       dma(2, seqs), dma(2, 7), dma(1, 7), dma(2, 4), dma(2, 7), dma(1, 7), dma(4, 2), dma(3, 2, 2)]
             args = [enc_lens, mixed.reshape(rows, D), res, norm_cross, norm_mlp]
-            weights = [caches[2], caches[3], pack, ypack, xtail, w_gate, w_up, w_down]
+            weights = [caches[2], caches[3], mid, xtail, w_out, w_cquery, w_cout, w_gate, w_up, w_down]
             if last:
                 hid, = exchange_call(
-                    functools.partial(layer_kernel, l, True, seqs), 1 + l, "last", "svvvv" + "h" * 8,
-                    args + weights, [res_t],
+                    functools.partial(layer_kernel, l, True, seqs), 1 + l, "last", "svvvv" + "h" * 10,
+                    args + weights, [hid_t],
                     scratch + [rowbuf(D), rowbuf(half), vm((2, rows, half), F32)], 20_000_000_000)
             else:
-                scratch += [rowbuf(D, F32), colbuf(half), vm((depth, 3 * half)), rowbuf(3 * half)] + coming
-                scratch += [dma(3, 7), dma(3, 3), dma(3, 2)]
-                res, qkv, pack, tail_own = exchange_call(
-                    functools.partial(layer_kernel, l, False, seqs), 1 + l, "layer", "svvvvv" + "h" * 14,
-                    args + [norm_self] + weights
-                    + [w_query, w_key, w_value, w_out, w_cquery, w_cout],
-                    [res_t, qkv_t, pack_t, tail_t], scratch, 20_000_000_000)
+                scratch += [rowbuf(D), colbuf(half), vm((depth, 3 * half)), rowbuf(3 * half)] + coming
+                scratch += [dma(3, 7), dma(4), dma(2, 2)]
+                res, qkv, mid, tail_own = exchange_call(
+                    functools.partial(layer_kernel, l, False, seqs), 1 + l, "layer", "svvvvv" + "h" * 13,
+                    args + [norm_self] + weights + [w_query, w_key, w_value],
+                    [res_t, qkv_t, mid_t, tail_t], scratch, 20_000_000_000)
 
         def unflat(cache):
             return jnp.transpose(cache.reshape(layers, seqs, HEADS, HEAD_DIM, cache_len), (0, 1, 4, 2, 3))

time: 132 us -> 136 us (1.030)
  Pallas kernels: 125 us -> 129 us
  starting transfers between devices: 4.71 us -> 2.21 us
  waiting for transfers between devices: 0.01 us -> 1.99 us
    pallas_call x3, Pallas kernels: 86.6 us -> 91 us  [exchange_call(): pl.pallas_call(kernel, out_shape=tuple((t for _, t in outs)), in_specs=sp...]
    ppermute x2 -> x0, starting transfers between devices: 2.89 us -> none  [local_step(): ypack = lax.ppermute(pack, 'col', flip)]
    ppermute x2, waiting for transfers between devices: 0.01 us -> 1.99 us  [local_step(): xtail = lax.ppermute(tail_own, 'row', across)]
  transfers between devices with their start and end apart: 4 -> 2, of which waited for: 0 -> 1; matrix products, arithmetic and copies ran while one was open for 0% -> 0% of each run, Pallas kernels for 29% -> 28%
where the time goes in v3:
time: 136 us; the launch traced here: 135 us
  Pallas kernels  129 us (95%)
  starting transfers between devices  2.21 us (2%)
  waiting for transfers between devices  1.99 us (1%)
  other arithmetic  1.52 us (1%)
    pallas_call x3, Pallas kernels, exchange_call(): pl.pallas_call(kernel, out_shape=tuple((t for _, t in outs)), in_specs=sp...  91 us
    pallas_call x2, Pallas kernels, self_attention(): pl.pallas_call(functools.partial(self_kernel, layer, seqs, outs is not No...  38.1 us
  transfers between devices with their start and end apart: 2, of which 1 were waited for; matrix products, arithmetic and copies ran while one was open for 0% of the time, Pallas kernels for 28%

profile of v3, /device:TPU:0, one launch (start us, length us, event | category | flops | bytes accessed | tf_op | source)
XLA Modules:
  0.0 135.4 jit_solution(7949957781813239673)
XLA Ops:
  0.6 23.0 %start.1 = (f32[64,768]{1,0:T(8,128)}, f32[2,32,1152]{2,1,0:T(8,128)}, bf16[192,768]{1,0:T(8,128)(2,1)}, bf16[192,2432]{1,0:T(8,128)(2,1)}, f32[16,512]{1,0:T(8,128)}) custom-call(bf16[16,768]{1,0:T(8,128)(2,1)} %first_ref.1, bf16[16,768]{1,0:T(8,128)(2,1)} %second_ref.1, bf16[2,768]{1,0:T(2,128)(2,1)} %refs_0_.1, f32[12,32]{1,0:T(8,128)} %bitcast.34, ...), custom_call_target="tpu_custom_call" | custom-call | flops 3000000000 | bytes 8388608 | tf_op jit(solution)/shard_map/start/pallas_call | solution.py:499
  23.6 1.1 collective-permute-start
  24.7 19.0 %self_attn.2 = (bf16[2,16,768,512]{3,2,1,0:T(8,128)(2,1)}, bf16[2,16,768,512]{3,2,1,0:T(8,128)(2,1)}, f32[2,16,768]{2,1,0:T(8,128)}) custom-call(s32[16]{0:T(128)} %pos_ref.3, f32[2,32,1152]{2,1,0:T(8,128)} %get-tuple-element.18.qkv_ref, f32[16,512]{1,0:T(8,128)} %get-tuple-element.19.tab_ref, bf16[2,16,768,512]{3,2,1,0:T(8,128)(2,1)} %bitcast.22, ...), custom_call_target="tpu_custom_call" | custom-call | flops 20000000000 | bytes 50331648 | tf_op jit(solution)/shard_map/self_attn/pallas_call | solution.py:143
  43.7 2.0 %collective-permute-done.refs_4_ = bf16[192,2432]{1,0:T(8,128)(2,1)} collective-permute-done((bf16[192,2432]{1,0:T(8,128)(2,1)}, bf16[192,2432]{1,0:T(8,128)(2,1)}, u32[]{:S(2)}, u32[]{:S(2)}) %collective-permute-start) | collective-permute-done | bytes 933920 | tf_op jit(solution)/shard_map/ppermute | solution.py:552
  45.7 36.2 %layer.1 = (f32[64,768]{1,0:T(8,128)}, f32[2,32,1152]{2,1,0:T(8,128)}, bf16[192,768]{1,0:T(8,128)(2,1)}, bf16[192,2432]{1,0:T(8,128)(2,1)}) custom-call(s32[16]{0:T(128)} %len_ref.3, f32[32,768]{1,0:T(8,128)} %bitcast.35, f32[64,768]{1,0:T(8,128)} %get-tuple-element.21.x_ref, bf16[2,768]{1,0:T(2,128)(2,1)} %gcross_ref.3, bf16[2,768]{1,0:T(2,128)(2,1)} %gmlp_ref.3, ...), custom_call_target="tpu_custom_call" | custom-call | flops 20000000000 | bytes 8388608 | tf_op jit(solution)/shard_map/layer/pallas_call | solution.py:499
  82.0 1.1 collective-permute-start.1
  83.1 19.0 %self_attn.3 = (bf16[2,16,768,512]{3,2,1,0:T(8,128)(2,1)}, bf16[2,16,768,512]{3,2,1,0:T(8,128)(2,1)}, f32[2,16,768]{2,1,0:T(8,128)}) custom-call(s32[16]{0:T(128)} %pos_ref.3, f32[2,32,1152]{2,1,0:T(8,128)} %get-tuple-element.24.qkv_ref, f32[16,512]{1,0:T(8,128)} %get-tuple-element.19.tab_ref, ...), custom_call_target="tpu_custom_call", output_to_operand_aliasing={{0}: (5, {}), {1}: (6, {})} | custom-call | flops 20000000000 | bytes 50331648 | tf_op jit(solution)/shard_map/self_attn/pallas_call | solution.py:143
  102.1 0.0 collective-permute-done.1.refs_3_
  102.1 31.8 %last.1 = f32[32,768]{1,0:T(8,128)} custom-call(s32[16]{0:T(128)} %len_ref.3, f32[32,768]{1,0:T(8,128)} %bitcast.33, f32[64,768]{1,0:T(8,128)} %get-tuple-element.28.x_ref, bf16[2,768]{1,0:T(2,128)(2,1)} %gcross_ref.3, bf16[2,768]{1,0:T(2,128)(2,1)} %gmlp_ref.3, bf16[2,16,768,512]{3,2,1,0:T(8,128)(2,1)} %bitcast.30, bf16[2,16,768,512]{3,2,1,0:T(8,128)(2,1)} %bitcast.32, ...), custom_call_target="tpu_custom_call" | custom-call | flops 20000000000 | bytes 8388608 | tf_op jit(solution)/shard_map/last/pallas_call | solution.py:499
  133.9 1.5 %convert_element_type.6 = bf16[32,768]{1,0:T(8,128)(2,1)} convert(f32[32,768]{1,0:T(8,128)} %last.1) | non-fusion elementwise | flops 24576 | bytes 147456 | tf_op jit(solution)/shard_map/convert_element_type | solution.py:578
Async XLA Ops:
  23.6 22.1 %collective-permute-start = (bf16[192,2432]{1,0:T(8,128)(2,1)}, bf16[192,2432]{1,0:T(8,128)(2,1)}, u32[]{:S(2)}, u32[]{:S(2)}) collective-permute-start(bf16[192,2432]{1,0:T(8,128)(2,1)} %get-tuple-element.23), channel_id=1, source_target_pairs={{0,2},{1,3},{2,0},{3,1},{4,6},{5,7},{6,4},{7,5}} | collective-permute-start | bytes 2801672 | tf_op jit(solution)/shard_map/ppermute | solution.py:552
  82.0 20.1 %collective-permute-start.1 = (bf16[192,2432]{1,0:T(8,128)(2,1)}, bf16[192,2432]{1,0:T(8,128)(2,1)}, u32[]{:S(2)}, u32[]{:S(2)}) collective-permute-start(bf16[192,2432]{1,0:T(8,128)(2,1)} %get-tuple-element.30), channel_id=1, source_target_pairs={{0,2},{1,3},{2,0},{3,1},{4,6},{5,7},{6,4},{7,5}} | collective-permute-start | bytes 2801672 | tf_op jit(solution)/shard_map/ppermute | solution.py:552

commit v4 on v2

--- a/solution.py
+++ b/solution.py
@@ -169,12 +169,13 @@
         self.peer = (dp, 1 - self.c, self.r)
         self.partner = (dp, self.c, core)
         self.xpeer = (dp, self.c, self.across)
+        self.diagonal = (dp, 1 - self.c, self.across)
 
     def greet(self):
         barrier = pltpu.get_barrier_semaphore()
-        for other in (self.peer, self.partner, self.xpeer):
+        for other in (self.peer, self.partner, self.xpeer, self.diagonal):
             pl.semaphore_signal(barrier, inc=1, device_id=other, device_id_type=MESH)
-        pl.semaphore_wait(barrier, 3)
+        pl.semaphore_wait(barrier, 4)
 
     def remote(self, src, dst, send_sem, recv_sem, to):
         return pltpu.make_async_remote_copy(src_ref=src, dst_ref=dst, send_sem=send_sem, recv_sem=recv_sem,
@@ -189,16 +190,6 @@
         buf[0] = own
         self.send(buf.at[0], buf.at[1], sems).wait()
         return jnp.concatenate([buf[0], buf[1]], axis=0)
-
-    def trade_columns(self, mine, buf, sems):
-        rows, width = mine.shape[0] // 2, mine.shape[1]
-        c = self.c
-        buf[c] = mine.astype(BF16).reshape(2, rows, width)
-        first = self.send(buf.at[c, 0], buf.at[c, 1], sems.at[0])
-        second = self.send(buf.at[c, 1], buf.at[c, 0], sems.at[1])
-        first.wait()
-        second.wait()
-        return jnp.concatenate([buf[0].reshape(2 * rows, width), buf[1].reshape(2 * rows, width)], axis=1)
 
     def give_rows(self, mine, buf, sems, out_ref):
         rows = mine.shape[0] // 2
@@ -318,6 +309,48 @@
     def finish(self, w):
         each(self.locals[w], "wait")
         each(self.shares[w], "wait")
+
+
+class Down:
+    def __init__(self, st, own, dst, sems):
+        depth = own.shape[0]
+        x, core = st.r // 2, st.r % 2
+        at = pl.ds(pl.multiple_of(core * depth, depth), depth)
+        self.home = x == st.c
+        dp = lax.axis_index("dp")
+        place = dst.at[st.c, at, :]
+        self.local = pltpu.make_async_copy(own, place, sems.at[0, st.c])
+        self.near = st.remote(own, place, sems.at[1, 0], sems.at[0, st.c], (dp, x, st.r))
+        self.far = st.remote(own, place, sems.at[1, 1], sems.at[0, st.c], (dp, x, st.across))
+        self.arrive, self.relays = [], []
+        for cb in range(2):
+            got = dst.at[cb, at, :]
+            self.arrive.append(st.remote(own, got, sems.at[1, 0], sems.at[0, cb], st.peer))
+            self.relays.append(st.remote(got, got, sems.at[2, cb], sems.at[3, cb], st.partner))
+
+    def open(self):
+        self.far.start()
+
+        @pl.when(self.home)
+        def _():
+            self.local.start()
+
+        @pl.when(jnp.logical_not(self.home))
+        def _():
+            self.near.start()
+
+    def relay(self):
+        for arrive, relay in zip(self.arrive, self.relays):
+            arrive.wait_recv()
+            relay.start()
+
+    def finish(self):
+        self.far.wait_send()
+
+        @pl.when(jnp.logical_not(self.home))
+        def _():
+            self.near.wait_send()
+        each(self.relays, "wait")
 
 
 class NextLayer:
@@ -385,17 +418,17 @@
 def layer_kernel(layer, last, seqs, len_ref, o_ref, x_ref, gcross_ref, gmlp_ref, *refs):
     if last:
         (ck, cv, pack_in, ypack_in, xtail_in, wg_r, wu_r, wd_r, hid_ref,
-         kbuf, vbuf, wattn, wtail, wdown, qs, os, ubuf, kvsem, asem, wtsem, dsem, sem, sem2, rbuf, zbuf, zs) = refs
+         kbuf, vbuf, wattn, wtail, wdown, qs, os, nbuf, zbuf, kvsem, asem, wtsem, dsem, sem, sem2) = refs
     else:
         (gself_ref, ck, cv, pack_in, ypack_in, xtail_in, wg_r, wu_r, wd_r, wq_r, wk_r, wv_r, wo_r, wc_r, wco_r,
          x_out, qkv_ref, pack_ref, tail_ref,
-         kbuf, vbuf, wattn, wtail, wdown, qs, os, ubuf, kvsem, asem, wtsem, dsem, sem, sem2,
-         rbuf, zbuf, wqkv, qkvbuf, pbuf, tbuf, wsem, nsem, xsem) = refs
+         kbuf, vbuf, wattn, wtail, wdown, qs, os, nbuf, zbuf, kvsem, asem, wtsem, dsem, sem, sem2,
+         rbuf, wqkv, qkvbuf, pbuf, tbuf, wsem, nsem, xsem) = refs
     st = Stage()
     rows = o_ref.shape[0]
     attn = Whole(st, (pack_in, ypack_in), wattn, asem)
     tail = weights_of(st, (wg_r, wu_r), layer, wtail, wtsem, xtail_in)
-    down = weights_of(st, (wd_r,), layer, wdown, dsem)
+    down = Down(st, wd_r.at[layer], wdown, dsem)
     attn.open_local()
 
     def caches(b):
@@ -408,10 +441,9 @@
 
     st.greet()
     attn.open_share()
-    each(down, "open_cross")
+    down.open()
     lax.fori_loop(0, seqs, fetch_caches, 0)
     each(tail, "open_local")
-    each(down, "open_local")
     if not last:
         ahead = weights_of(st, (wq_r, wk_r, wv_r), layer + 1, wqkv, wsem)
         coming = NextLayer(st, (wo_r, wc_r, wco_r), (wg_r, wu_r), layer + 1, pack_ref, tail_ref, pbuf, tbuf,
@@ -427,7 +459,6 @@
     for cb, q in enumerate(both_blocks(rms(res, gcross_ref[layer:layer + 1, :]), wattn, 1)):
         qs[cb] = q.astype(F32)
     each(tail, "open_share")
-    each(down, "open_share")
     if not last:
         each(ahead, "open_share")
         coming.store()
@@ -445,7 +476,7 @@
         return carry
 
     lax.fori_loop(0, seqs // SEQ_BLOCK, cross_step, 0)
-    each(down, "relay")
+    down.relay()
     attn.finish(2)
     y = jnp.concatenate(both_blocks(os[...].reshape(rows, D).astype(BF16), wattn, 2), axis=1)
     res = res + y.astype(F32)
@@ -458,28 +489,30 @@
         return (gate * jax.nn.sigmoid(gate) * up).astype(BF16)
 
     normed = rms(res, gain)
-    rbuf[0] = normed if last else res
-    moving = st.send(rbuf.at[0], rbuf.at[1], sem.at[0])
+    nbuf[0] = normed
+    moving = st.send(nbuf.at[0], nbuf.at[1], sem.at[0])
+    if not last:
+        rbuf[0] = res
+        moving_res = st.send(rbuf.at[0], rbuf.at[1], sem2.at[0, 0])
     each(tail, "finish")
-    ubuf[st.c, 0] = gated(normed)
-    moving_own = st.send(ubuf.at[st.c, 0], ubuf.at[st.c, 1], sem2.at[0, 0])
+    own_act = gated(normed)
     moving.wait()
-    ubuf[st.c, 1] = gated(rbuf[1] if last else rms(rbuf[1], gain))
-    moving_other = st.send(ubuf.at[st.c, 1], ubuf.at[st.c, 0], sem2.at[0, 1])
+    act = jnp.concatenate([own_act, gated(nbuf[1])], axis=0)
+    down.finish()
+    part = jnp.concatenate([dot32(act, wdown[0]), dot32(act, wdown[1])], axis=1)
+    zbuf[0, 0] = part[:rows]
+    zbuf[0, 1] = part[rows:]
+    moving_z = [st.send(zbuf.at[0, 1], zbuf.at[1, 0], sem2.at[1, 0])]
     if not last:
-        res = jnp.concatenate([res, rbuf[1]], axis=0)
-    moving_own.wait()
-    moving_other.wait()
-    act = jnp.concatenate([ubuf[0].reshape(2 * rows, ff), ubuf[1].reshape(2 * rows, ff)], axis=1)
-    if not last:
+        moving_z.append(st.send(zbuf.at[0, 0], zbuf.at[1, 1], sem2.at[1, 1]))
         each(ahead, "relay")
-    each(down, "finish")
-    z = dot32(act, wdown[...])
+        moving_res.wait()
+    each(moving_z, "wait")
     if last:
-        st.give_rows(z, zbuf, sem.at[1], zs)
-        hid_ref[...] = res + jnp.concatenate([zs[0], zs[1]], axis=1)
+        hid_ref[...] = res + (zbuf[0, 0] + zbuf[1, 0]).astype(BF16).astype(F32)
     else:
-        res = res + st.trade_columns(z, zbuf, sem2.at[1]).astype(F32)
+        z = (zbuf[0] + zbuf[1]).astype(BF16).astype(F32)
+        res = jnp.concatenate([res + z[0], rbuf[1] + z[1]], axis=0)
         x_out[...] = res[:rows]
         normed = rms(res, gself_ref[layer + 1:layer + 2, :])
         each(ahead, "finish")
@@ -524,7 +557,6 @@
         vm = lambda shape, dt=BF16: pltpu.VMEM(shape, dt)
         dma = lambda *shape: pltpu.SemaphoreType.DMA(shape)
         rowbuf = lambda width, dt=BF16: vm((2, rows, width), dt)
-        colbuf = lambda width: vm((2, 2, rows, width))
         res_t = ("v", jax.ShapeDtypeStruct((rows, D), F32))
         qkv_t = ("v", jax.ShapeDtypeStruct((2, rows, 3 * half), F32))
         pack_t = ("h", jax.ShapeDtypeStruct((2, block, 3 * half), BF16))
@@ -548,18 +580,18 @@
             k_out, v_out, mixed = self_attention(l, start_pos, qkv, table, caches[0], caches[1], outs)
             outs = (k_out, v_out)
             cache_buf = vm((seqs, D, cross_k.shape[2]))
-            scratch = [cache_buf, cache_buf, vm((2, depth, 3 * half)), vm((depth, 2 * ffc)), vm((fdepth, half)),
-                       vm((2, rows, half), F32), vm((TOKENS, seqs, D), F32), colbuf(ffc),
-                       dma(2, seqs), dma(3, 2, 2, 3), dma(2, 7), dma(1, 7), dma(2, 2), dma(2, 2, 2)]
+            scratch = [cache_buf, cache_buf, vm((2, depth, 3 * half)), vm((depth, 2 * ffc)), vm((2, fdepth // 2, half)),
+                       vm((2, rows, half), F32), vm((TOKENS, seqs, D), F32), rowbuf(D), vm((2, 2, rows, D), F32),
+                       dma(2, seqs), dma(3, 2, 2, 3), dma(2, 7), dma(4, 2), dma(2, 2), dma(2, 2, 2)]
             args = [enc_lens, mixed.reshape(rows, D), res, norm_cross, norm_mlp]
             weights = [caches[2], caches[3], pack, ypack, xtail, w_gate, w_up, w_down]
             if last:
                 hid, = exchange_call(
                     functools.partial(layer_kernel, l, True, seqs), 1 + l, "last", "svvvv" + "h" * 8,
                     args + weights, [res_t],
-                    scratch + [rowbuf(D), rowbuf(half), vm((2, rows, half), F32)], 20_000_000_000)
+                    scratch, 20_000_000_000)
             else:
-                scratch += [rowbuf(D, F32), colbuf(half), vm((depth, 3 * half)), rowbuf(3 * half)] + coming
+                scratch += [rowbuf(D, F32), vm((depth, 3 * half)), rowbuf(3 * half)] + coming
                 scratch += [dma(3, 7), dma(3, 3), dma(3, 2)]
                 res, qkv, pack, tail_own = exchange_call(
                     functools.partial(layer_kernel, l, False, seqs), 1 + l, "layer", "svvvvv" + "h" * 14,

time: 132 us -> 126 us (0.955)
  Pallas kernels: 125 us -> 119 us
    pallas_call x3, Pallas kernels: 86.6 us -> 80.9 us  [exchange_call(): pl.pallas_call(kernel, out_shape=tuple((t for _, t in outs)), in_specs=sp...]
    ppermute x2, starting transfers between devices: 2.89 us -> 1.19 us  [local_step(): ypack = lax.ppermute(pack, 'col', flip)]
  transfers between devices with their start and end apart: 4 -> 4, of which waited for: 0 -> 1; matrix products, arithmetic and copies ran while one was open for 0% -> 0% of each run, Pallas kernels for 29% -> 30%
where the time goes in v4:
time: 126 us
  Pallas kernels  119 us (94%)
  starting transfers between devices  4.16 us (3%)
  other arithmetic  1.52 us (1%)
    pallas_call x3, Pallas kernels, exchange_call(): pl.pallas_call(kernel, out_shape=tuple((t for _, t in outs)), in_specs=sp...  80.9 us
    pallas_call x2, Pallas kernels, self_attention(): pl.pallas_call(functools.partial(self_kernel, layer, seqs, outs is not No...  38.1 us
    ppermute x2, starting transfers between devices, local_step(): xtail = lax.ppermute(tail_own, 'row', across)  2.97 us
  transfers between devices with their start and end apart: 4, of which 1 were waited for; matrix products, arithmetic and copies ran while one was open for 0% of the time, Pallas kernels for 30%

profile of v4, /device:TPU:0, one launch (start us, length us, event | category | flops | bytes accessed | tf_op | source)
XLA Modules:
  0.0 126.1 jit_solution(14503357649963604359)
XLA Ops:
  0.6 26.1 %start.1 = (f32[32,768]{1,0:T(8,128)}, f32[2,32,1152]{2,1,0:T(8,128)}, bf16[2,192,1152]{2,1,0:T(8,128)(2,1)}, bf16[192,2048]{1,0:T(8,128)(2,1)}, f32[16,512]{1,0:T(8,128)}) custom-call(bf16[16,768]{1,0:T(8,128)(2,1)} %first_ref.1, bf16[16,768]{1,0:T(8,128)(2,1)} %second_ref.1, bf16[2,768]{1,0:T(2,128)(2,1)} %refs_0_.1, f32[12,32]{1,0:T(8,128)} %bitcast.34, ...), custom_call_target="tpu_custom_call" | custom-call | flops 3000000000 | bytes 8388608 | tf_op jit(solution)/shard_map/start/pallas_call | solution.py:526
  26.8 1.5 %collective-permute-start.1 = (bf16[192,2048]{1,0:T(8,128)(2,1)}, bf16[192,2048]{1,0:T(8,128)(2,1)}, u32[]{:S(2)}, u32[]{:S(2)}) collective-permute-start(bf16[192,2048]{1,0:T(8,128)(2,1)} %get-tuple-element.23), channel_id=1, source_target_pairs={{0,2},{1,3},{2,0},{3,1},{4,6},{5,7},{6,4},{7,5}} | collective-permute-start | bytes 2359304 | tf_op jit(solution)/shard_map/ppermute | solution.py:579
  28.3 0.6 collective-permute-start
  28.8 19.1 %self_attn.2 = (bf16[2,16,768,512]{3,2,1,0:T(8,128)(2,1)}, bf16[2,16,768,512]{3,2,1,0:T(8,128)(2,1)}, f32[2,16,768]{2,1,0:T(8,128)}) custom-call(s32[16]{0:T(128)} %pos_ref.3, f32[2,32,1152]{2,1,0:T(8,128)} %get-tuple-element.18.qkv_ref, f32[16,512]{1,0:T(8,128)} %get-tuple-element.19.tab_ref, bf16[2,16,768,512]{3,2,1,0:T(8,128)(2,1)} %bitcast.22, ...), custom_call_target="tpu_custom_call" | custom-call | flops 20000000000 | bytes 50331648 | tf_op jit(solution)/shard_map/self_attn/pallas_call | solution.py:143
  47.9 0.0 collective-permute-done.1.refs_5_
  47.9 0.7 collective-permute-done.refs_4_
  48.6 32.8 %layer.1 = (f32[32,768]{1,0:T(8,128)}, f32[2,32,1152]{2,1,0:T(8,128)}, bf16[2,192,1152]{2,1,0:T(8,128)(2,1)}, bf16[192,2048]{1,0:T(8,128)(2,1)}) custom-call(s32[16]{0:T(128)} %len_ref.3, f32[32,768]{1,0:T(8,128)} %bitcast.35, f32[32,768]{1,0:T(8,128)} %get-tuple-element.21.x_ref, bf16[2,768]{1,0:T(2,128)(2,1)} %gcross_ref.3, bf16[2,768]{1,0:T(2,128)(2,1)} %gmlp_ref.3, ...), custom_call_target="tpu_custom_call" | custom-call | flops 20000000000 | bytes 8388608 | tf_op jit(solution)/shard_map/layer/pallas_call | solution.py:526
  81.4 1.5 %collective-permute-start.3 = (bf16[192,2048]{1,0:T(8,128)(2,1)}, bf16[192,2048]{1,0:T(8,128)(2,1)}, u32[]{:S(2)}, u32[]{:S(2)}) collective-permute-start(bf16[192,2048]{1,0:T(8,128)(2,1)} %get-tuple-element.30), channel_id=1, source_target_pairs={{0,2},{1,3},{2,0},{3,1},{4,6},{5,7},{6,4},{7,5}} | collective-permute-start | bytes 2359304 | tf_op jit(solution)/shard_map/ppermute | solution.py:579
  82.9 0.6 collective-permute-start.2
  83.5 19.0 %self_attn.3 = (bf16[2,16,768,512]{3,2,1,0:T(8,128)(2,1)}, bf16[2,16,768,512]{3,2,1,0:T(8,128)(2,1)}, f32[2,16,768]{2,1,0:T(8,128)}) custom-call(s32[16]{0:T(128)} %pos_ref.3, f32[2,32,1152]{2,1,0:T(8,128)} %get-tuple-element.24.qkv_ref, f32[16,512]{1,0:T(8,128)} %get-tuple-element.19.tab_ref, ...), custom_call_target="tpu_custom_call", output_to_operand_aliasing={{0}: (5, {}), {1}: (6, {})} | custom-call | flops 20000000000 | bytes 50331648 | tf_op jit(solution)/shard_map/self_attn/pallas_call | solution.py:143
  102.6 0.0 collective-permute-done.3.refs_4_
  102.6 0.0 collective-permute-done.2.refs_3_
  102.6 22.0 %last.1 = f32[32,768]{1,0:T(8,128)} custom-call(s32[16]{0:T(128)} %len_ref.3, f32[32,768]{1,0:T(8,128)} %bitcast.33, f32[32,768]{1,0:T(8,128)} %get-tuple-element.28.x_ref, bf16[2,768]{1,0:T(2,128)(2,1)} %gcross_ref.3, bf16[2,768]{1,0:T(2,128)(2,1)} %gmlp_ref.3, bf16[2,16,768,512]{3,2,1,0:T(8,128)(2,1)} %bitcast.30, bf16[2,16,768,512]{3,2,1,0:T(8,128)(2,1)} %bitcast.32, ...), custom_call_target="tpu_custom_call" | custom-call | flops 20000000000 | bytes 8388608 | tf_op jit(solution)/shard_map/last/pallas_call | solution.py:526
  124.6 1.5 %convert_element_type.6 = bf16[32,768]{1,0:T(8,128)(2,1)} convert(f32[32,768]{1,0:T(8,128)} %last.1) | non-fusion elementwise | flops 24576 | bytes 147456 | tf_op jit(solution)/shard_map/convert_element_type | solution.py:605
Async XLA Ops:
  26.8 21.1 %collective-permute-start.1 = (bf16[192,2048]{1,0:T(8,128)(2,1)}, bf16[192,2048]{1,0:T(8,128)(2,1)}, u32[]{:S(2)}, u32[]{:S(2)}) collective-permute-start(bf16[192,2048]{1,0:T(8,128)(2,1)} %get-tuple-element.23), channel_id=1, source_target_pairs={{0,2},{1,3},{2,0},{3,1},{4,6},{5,7},{6,4},{7,5}} | collective-permute-start | bytes 2359304 | tf_op jit(solution)/shard_map/ppermute | solution.py:579
  28.3 20.4 %collective-permute-start = (bf16[2,192,1152]{2,1,0:T(8,128)(2,1)}, bf16[2,192,1152]{2,1,0:T(8,128)(2,1)}, u32[]{:S(2)}, u32[]{:S(2)}) collective-permute-start(bf16[2,192,1152]{2,1,0:T(8,128)(2,1)} %get-tuple-element.22.refs_3_), channel_id=1, source_target_pairs={{0,4},{4,0},{1,5},{5,1},{2,6},{6,2},{3,7},{7,3}} | collective-permute-start | bytes 2654216 | tf_op jit(solution)/shard_map/ppermute | solution.py:578
  81.4 21.2 %collective-permute-start.3 = (bf16[192,2048]{1,0:T(8,128)(2,1)}, bf16[192,2048]{1,0:T(8,128)(2,1)}, u32[]{:S(2)}, u32[]{:S(2)}) collective-permute-start(bf16[192,2048]{1,0:T(8,128)(2,1)} %get-tuple-element.30), channel_id=1, source_target_pairs={{0,2},{1,3},{2,0},{3,1},{4,6},{5,7},{6,4},{7,5}} | collective-permute-start | bytes 2359304 | tf_op jit(solution)/shard_map/ppermute | solution.py:579
  82.9 19.7 %collective-permute-start.2 = (bf16[2,192,1152]{2,1,0:T(8,128)(2,1)}, bf16[2,192,1152]{2,1,0:T(8,128)(2,1)}, u32[]{:S(2)}, u32[]{:S(2)}) collective-permute-start(bf16[2,192,1152]{2,1,0:T(8,128)(2,1)} %get-tuple-element.29.refs_2_), channel_id=1, source_target_pairs={{0,4},{4,0},{1,5},{5,1},{2,6},{6,2},{3,7},{7,3}} | collective-permute-start | bytes 2654216 | tf_op jit(solution)/shard_map/ppermute | solution.py:578

commit v5 on v4

--- a/solution.py
+++ b/solution.py
@@ -171,11 +171,11 @@
         self.xpeer = (dp, self.c, self.across)
         self.diagonal = (dp, 1 - self.c, self.across)
 
-    def greet(self):
+    def greet(self, *others):
         barrier = pltpu.get_barrier_semaphore()
-        for other in (self.peer, self.partner, self.xpeer, self.diagonal):
+        for other in others:
             pl.semaphore_signal(barrier, inc=1, device_id=other, device_id_type=MESH)
-        pl.semaphore_wait(barrier, 4)
+        pl.semaphore_wait(barrier, len(others))
 
     def remote(self, src, dst, send_sem, recv_sem, to):
         return pltpu.make_async_remote_copy(src_ref=src, dst_ref=dst, send_sem=send_sem, recv_sem=recv_sem,
@@ -203,15 +203,16 @@
 
 
 class Weight:
-    def __init__(self, st, own, dst, col, sems, crossed=None):
+    def __init__(self, st, own, dst, col, sems, crossed=None, staged=False):
         depth, width = own.shape
-        self.st, self.crossed = st, crossed
+        self.st, self.crossed, self.staged = st, crossed, staged
 
         def place(owner):
             return dst.at[pl.ds(pl.multiple_of(owner * depth, depth), depth), pl.ds(col, width)]
 
         mine, theirs = place(st.r), place(st.across)
         self.local = pltpu.make_async_copy(own, mine, sems.at[0])
+        own = mine if staged else own
         self.share = st.remote(own, mine, sems.at[1], sems.at[2], st.partner)
         if crossed is None:
             self.cross = st.remote(own, mine, sems.at[3], sems.at[4], st.xpeer)
@@ -226,6 +227,8 @@
             self.cross.start()
 
     def open_cross(self):
+        if self.staged:
+            self.local.wait()
         if self.crossed is None:
             self.cross.start()
 
@@ -240,7 +243,8 @@
             self.pass_on.start()
 
     def finish(self):
-        self.local.wait()
+        if not self.staged:
+            self.local.wait()
         self.share.wait()
         if self.crossed is None:
             self.cross.wait_send()
@@ -254,12 +258,12 @@
         getattr(item, name)()
 
 
-def weights_of(st, refs, layer, dst, sems, crossed=None):
+def weights_of(st, refs, layer, dst, sems, crossed=None, staged=False):
     col, found = 0, []
     for n, ref in enumerate(refs):
         width = ref.shape[2]
         given = None if crossed is None else crossed.at[:, pl.ds(col, width)]
-        found.append(Weight(st, ref.at[layer], dst, col, sems.at[n], given))
+        found.append(Weight(st, ref.at[layer], dst, col, sems.at[n], given, staged))
         col += width
     return found
 
@@ -312,23 +316,25 @@
 
 
 class Down:
-    def __init__(self, st, own, dst, sems):
+    def __init__(self, st, own, dst, stage, sems):
         depth = own.shape[0]
+        self.load = pltpu.make_async_copy(own, stage, sems.at[4, 0])
         x, core = st.r // 2, st.r % 2
         at = pl.ds(pl.multiple_of(core * depth, depth), depth)
         self.home = x == st.c
         dp = lax.axis_index("dp")
         place = dst.at[st.c, at, :]
         self.local = pltpu.make_async_copy(own, place, sems.at[0, st.c])
-        self.near = st.remote(own, place, sems.at[1, 0], sems.at[0, st.c], (dp, x, st.r))
-        self.far = st.remote(own, place, sems.at[1, 1], sems.at[0, st.c], (dp, x, st.across))
+        self.near = st.remote(stage, place, sems.at[1, 0], sems.at[0, st.c], (dp, x, st.r))
+        self.far = st.remote(stage, place, sems.at[1, 1], sems.at[0, st.c], (dp, x, st.across))
         self.arrive, self.relays = [], []
         for cb in range(2):
             got = dst.at[cb, at, :]
-            self.arrive.append(st.remote(own, got, sems.at[1, 0], sems.at[0, cb], st.peer))
+            self.arrive.append(st.remote(stage, got, sems.at[1, 0], sems.at[0, cb], st.peer))
             self.relays.append(st.remote(got, got, sems.at[2, cb], sems.at[3, cb], st.partner))
 
     def open(self):
+        self.load.wait()
         self.far.start()
 
         @pl.when(self.home)
@@ -389,11 +395,11 @@
 def start_kernel(first_ref, second_ref, gain_ref, bias_ref, wq_r, wk_r, wv_r, wo_r, wc_r, wco_r, wg_r, wu_r,
                  x_ref, qkv_ref, pack_ref, tail_ref, tab_ref, hbuf, wqkv, qbuf, pbuf, tbuf, wsem, nsem, xsem, sem):
     st = Stage()
-    weights = weights_of(st, (wq_r, wk_r, wv_r), 0, wqkv, wsem)
+    weights = weights_of(st, (wq_r, wk_r, wv_r), 0, wqkv, wsem, staged=True)
     coming = NextLayer(st, (wo_r, wc_r, wco_r), (wg_r, wu_r), 0, pack_ref, tail_ref, pbuf, tbuf, nsem, xsem)
     each(weights, "open_local")
     each(coming.loads, "start")
-    st.greet()
+    st.greet(st.peer, st.partner, st.xpeer)
     each(weights, "open_cross")
     each(coming.sends, "start")
     each(weights, "open_share")
@@ -417,18 +423,18 @@
 
 def layer_kernel(layer, last, seqs, len_ref, o_ref, x_ref, gcross_ref, gmlp_ref, *refs):
     if last:
-        (ck, cv, pack_in, ypack_in, xtail_in, wg_r, wu_r, wd_r, hid_ref,
-         kbuf, vbuf, wattn, wtail, wdown, qs, os, nbuf, zbuf, kvsem, asem, wtsem, dsem, sem, sem2) = refs
+        (ck, cv, pack_in, ypack_in, xtail_in, wg_r, wu_r, wd_r, own_ref, zin_ref,
+         kbuf, vbuf, wattn, wtail, wdown, dstage, qs, os, nbuf, zbuf, kvsem, asem, wtsem, dsem, sem, sem2, rbuf, osem) = refs
     else:
         (gself_ref, ck, cv, pack_in, ypack_in, xtail_in, wg_r, wu_r, wd_r, wq_r, wk_r, wv_r, wo_r, wc_r, wco_r,
          x_out, qkv_ref, pack_ref, tail_ref,
-         kbuf, vbuf, wattn, wtail, wdown, qs, os, nbuf, zbuf, kvsem, asem, wtsem, dsem, sem, sem2,
+         kbuf, vbuf, wattn, wtail, wdown, dstage, qs, os, nbuf, zbuf, kvsem, asem, wtsem, dsem, sem, sem2,
          rbuf, wqkv, qkvbuf, pbuf, tbuf, wsem, nsem, xsem) = refs
     st = Stage()
     rows = o_ref.shape[0]
     attn = Whole(st, (pack_in, ypack_in), wattn, asem)
     tail = weights_of(st, (wg_r, wu_r), layer, wtail, wtsem, xtail_in)
-    down = Down(st, wd_r.at[layer], wdown, dsem)
+    down = Down(st, wd_r.at[layer], wdown, dstage, dsem)
     attn.open_local()
 
     def caches(b):
@@ -439,29 +445,29 @@
         each(caches(b), "start")
         return carry
 
-    st.greet()
+    down.load.start()
+    st.greet(st.peer, st.partner, st.xpeer, st.diagonal)
+    down.open()
     attn.open_share()
-    down.open()
     lax.fori_loop(0, seqs, fetch_caches, 0)
-    each(tail, "open_local")
     if not last:
         ahead = weights_of(st, (wq_r, wk_r, wv_r), layer + 1, wqkv, wsem)
         coming = NextLayer(st, (wo_r, wc_r, wco_r), (wg_r, wu_r), layer + 1, pack_ref, tail_ref, pbuf, tbuf,
                            nsem, xsem)
         each(ahead, "open_cross")
         each(coming.sends, "start")
-        each(ahead, "open_local")
-        each(coming.loads, "start")
     attn.finish(0)
     y = jnp.concatenate(both_blocks(o_ref[...].astype(BF16), wattn, 0), axis=1)
     res = x_ref[...] + y.astype(F32)
     attn.finish(1)
     for cb, q in enumerate(both_blocks(rms(res, gcross_ref[layer:layer + 1, :]), wattn, 1)):
         qs[cb] = q.astype(F32)
+    each(tail, "open_local")
     each(tail, "open_share")
     if not last:
+        each(ahead, "open_local")
+        each(coming.loads, "start")
         each(ahead, "open_share")
-        coming.store()
 
     def cross_step(i, carry):
         hmask = head_mask()
@@ -476,6 +482,8 @@
         return carry
 
     lax.fori_loop(0, seqs // SEQ_BLOCK, cross_step, 0)
+    if not last:
+        coming.store()
     down.relay()
     attn.finish(2)
     y = jnp.concatenate(both_blocks(os[...].reshape(rows, D).astype(BF16), wattn, 2), axis=1)
@@ -491,26 +499,36 @@
     normed = rms(res, gain)
     nbuf[0] = normed
     moving = st.send(nbuf.at[0], nbuf.at[1], sem.at[0])
-    if not last:
+    if last:
+        rbuf[...] = res
+        res_out = pltpu.make_async_copy(rbuf, own_ref.at[0], osem.at[0])
+        res_out.start()
+    else:
         rbuf[0] = res
         moving_res = st.send(rbuf.at[0], rbuf.at[1], sem2.at[0, 0])
     each(tail, "finish")
     own_act = gated(normed)
     moving.wait()
-    act = jnp.concatenate([own_act, gated(nbuf[1])], axis=0)
+    other_act = gated(nbuf[1])
     down.finish()
-    part = jnp.concatenate([dot32(act, wdown[0]), dot32(act, wdown[1])], axis=1)
-    zbuf[0, 0] = part[:rows]
-    zbuf[0, 1] = part[rows:]
-    moving_z = [st.send(zbuf.at[0, 1], zbuf.at[1, 0], sem2.at[1, 0])]
+
+    def partial_sum(act):
+        return jnp.concatenate([dot32(act, wdown[0]), dot32(act, wdown[1])], axis=1)
+
+    zbuf[0, 1] = partial_sum(other_act)
+    moving_z = [st.send(zbuf.at[0, 1], zin_ref if last else zbuf.at[1, 0], sem2.at[1, 0])]
+    zbuf[0, 0] = partial_sum(own_act)
     if not last:
         moving_z.append(st.send(zbuf.at[0, 0], zbuf.at[1, 1], sem2.at[1, 1]))
         each(ahead, "relay")
         moving_res.wait()
+    if last:
+        part_out = pltpu.make_async_copy(zbuf.at[0, 0], own_ref.at[1], osem.at[1])
+        part_out.start()
+        res_out.wait()
+        part_out.wait()
     each(moving_z, "wait")
-    if last:
-        hid_ref[...] = res + (zbuf[0, 0] + zbuf[1, 0]).astype(BF16).astype(F32)
-    else:
+    if not last:
         z = (zbuf[0] + zbuf[1]).astype(BF16).astype(F32)
         res = jnp.concatenate([res + z[0], rbuf[1] + z[1]], axis=0)
         x_out[...] = res[:rows]
@@ -580,16 +598,17 @@
             k_out, v_out, mixed = self_attention(l, start_pos, qkv, table, caches[0], caches[1], outs)
             outs = (k_out, v_out)
             cache_buf = vm((seqs, D, cross_k.shape[2]))
-            scratch = [cache_buf, cache_buf, vm((2, depth, 3 * half)), vm((depth, 2 * ffc)), vm((2, fdepth // 2, half)),
+            scratch = [cache_buf, cache_buf, vm((2, depth, 3 * half)), vm((depth, 2 * ffc)), vm((2, fdepth // 2, half)), vm((fdepth // 4, half)),
                        vm((2, rows, half), F32), vm((TOKENS, seqs, D), F32), rowbuf(D), vm((2, 2, rows, D), F32),
-                       dma(2, seqs), dma(3, 2, 2, 3), dma(2, 7), dma(4, 2), dma(2, 2), dma(2, 2, 2)]
+                       dma(2, seqs), dma(3, 2, 2, 3), dma(2, 7), dma(5, 2), dma(2, 2), dma(2, 2, 2)]
             args = [enc_lens, mixed.reshape(rows, D), res, norm_cross, norm_mlp]
             weights = [caches[2], caches[3], pack, ypack, xtail, w_gate, w_up, w_down]
             if last:
-                hid, = exchange_call(
+                own, zin = exchange_call(
                     functools.partial(layer_kernel, l, True, seqs), 1 + l, "last", "svvvv" + "h" * 8,
-                    args + weights, [res_t],
-                    scratch, 20_000_000_000)
+                    args + weights,
+                    [("h", jax.ShapeDtypeStruct((2, rows, D), F32)), ("h", jax.ShapeDtypeStruct((rows, D), F32))],
+                    scratch + [vm((rows, D), F32), dma(2)], 20_000_000_000)
             else:
                 scratch += [rowbuf(D, F32), vm((depth, 3 * half)), rowbuf(3 * half)] + coming
                 scratch += [dma(3, 7), dma(3, 3), dma(3, 2)]
@@ -602,6 +621,7 @@
         def unflat(cache):
             return jnp.transpose(cache.reshape(layers, seqs, HEADS, HEAD_DIM, cache_len), (0, 1, 4, 2, 3))
 
+        hid = own[0] + lax.reduce_precision(own[1] + zin, 8, 7)
         return hid.reshape(TOKENS, seqs, D).astype(BF16), unflat(outs[0]), unflat(outs[1])
 
     row_spec = P(batch_axes, None)

time: 126 us -> 126 us (level)
    ppermute x2, starting transfers between devices: 2.97 us -> 1.24 us  [local_step(): xtail = lax.ppermute(tail_own, 'row', across)]
    ppermute x2, starting transfers between devices: 1.19 us -> 2.74 us  [local_step(): ypack = lax.ppermute(pack, 'col', flip)]
  transfers between devices with their start and end apart: 4 -> 4, of which waited for: 1 -> 0; matrix products, arithmetic and copies ran while one was open for 0% -> 0% of each run, Pallas kernels for 30% -> 30%
where the time goes in v5:
time: 126 us; the launch traced here: 125 us
  Pallas kernels  119 us (94%)
  starting transfers between devices  3.98 us (3%)
  other arithmetic  1.63 us (1%)
    pallas_call x3, Pallas kernels, exchange_call(): pl.pallas_call(kernel, out_shape=tuple((t for _, t in outs)), in_specs=sp...  80.9 us
    pallas_call x2, Pallas kernels, self_attention(): pl.pallas_call(functools.partial(self_kernel, layer, seqs, outs is not No...  38.1 us
    ppermute x2, starting transfers between devices, local_step(): ypack = lax.ppermute(pack, 'col', flip)  2.74 us
  transfers between devices with their start and end apart: 4, of which 0 were waited for; matrix products, arithmetic and copies ran while one was open for 0% of the time, Pallas kernels for 30%

profile of v5, /device:TPU:0, one launch (start us, length us, event | category | flops | bytes accessed | tf_op | source)
XLA Modules:
  0.0 125.3 jit_solution(10774068042792994834)
XLA Ops:
  0.6 26.1 %start.1 = (f32[32,768]{1,0:T(8,128)}, f32[2,32,1152]{2,1,0:T(8,128)}, bf16[2,192,1152]{2,1,0:T(8,128)(2,1)}, bf16[192,2048]{1,0:T(8,128)(2,1)}, f32[16,512]{1,0:T(8,128)}) custom-call(bf16[16,768]{1,0:T(8,128)(2,1)} %first_ref.1, bf16[16,768]{1,0:T(8,128)(2,1)} %second_ref.1, bf16[2,768]{1,0:T(2,128)(2,1)} %refs_0_.1, f32[12,32]{1,0:T(8,128)} %bitcast.44, ...), custom_call_target="tpu_custom_call" | custom-call | flops 3000000000 | bytes 8388608 | tf_op jit(solution)/shard_map/start/pallas_call | solution.py:544
  26.8 0.6 collective-permute-start.1
  27.3 1.5 %collective-permute-start = (bf16[2,192,1152]{2,1,0:T(8,128)(2,1)}, bf16[2,192,1152]{2,1,0:T(8,128)(2,1)}, u32[]{:S(2)}, u32[]{:S(2)}) collective-permute-start(bf16[2,192,1152]{2,1,0:T(8,128)(2,1)} %get-tuple-element.24.refs_3_), channel_id=1, source_target_pairs={{0,4},{4,0},{1,5},{5,1},{2,6},{6,2},{3,7},{7,3}} | collective-permute-start | bytes 2654216 | tf_op jit(solution)/shard_map/ppermute | solution.py:596
  28.8 19.1 %self_attn.2 = (bf16[2,16,768,512]{3,2,1,0:T(8,128)(2,1)}, bf16[2,16,768,512]{3,2,1,0:T(8,128)(2,1)}, f32[2,16,768]{2,1,0:T(8,128)}) custom-call(s32[16]{0:T(128)} %pos_ref.3, f32[2,32,1152]{2,1,0:T(8,128)} %get-tuple-element.20.qkv_ref, f32[16,512]{1,0:T(8,128)} %get-tuple-element.21.tab_ref, bf16[2,16,768,512]{3,2,1,0:T(8,128)(2,1)} %bitcast.32, ...), custom_call_target="tpu_custom_call" | custom-call | flops 20000000000 | bytes 50331648 | tf_op jit(solution)/shard_map/self_attn/pallas_call | solution.py:143
  47.9 0.0 collective-permute-done.1.refs_5_
  47.9 0.0 collective-permute-done.refs_4_
  47.9 33.2 %layer.1 = (f32[32,768]{1,0:T(8,128)}, f32[2,32,1152]{2,1,0:T(8,128)}, bf16[2,192,1152]{2,1,0:T(8,128)(2,1)}, bf16[192,2048]{1,0:T(8,128)(2,1)}) custom-call(s32[16]{0:T(128)} %len_ref.3, f32[32,768]{1,0:T(8,128)} %bitcast.45, f32[32,768]{1,0:T(8,128)} %get-tuple-element.23.x_ref, bf16[2,768]{1,0:T(2,128)(2,1)} %gcross_ref.3, bf16[2,768]{1,0:T(2,128)(2,1)} %gmlp_ref.3, ...), custom_call_target="tpu_custom_call" | custom-call | flops 20000000000 | bytes 8388608 | tf_op jit(solution)/shard_map/layer/pallas_call | solution.py:544
  81.1 0.7 collective-permute-start.3
  81.8 1.2 collective-permute-start.2
  83.0 19.0 %self_attn.3 = (bf16[2,16,768,512]{3,2,1,0:T(8,128)(2,1)}, bf16[2,16,768,512]{3,2,1,0:T(8,128)(2,1)}, f32[2,16,768]{2,1,0:T(8,128)}) custom-call(s32[16]{0:T(128)} %pos_ref.3, f32[2,32,1152]{2,1,0:T(8,128)} %get-tuple-element.26.qkv_ref, f32[16,512]{1,0:T(8,128)} %get-tuple-element.21.tab_ref, ...), custom_call_target="tpu_custom_call", output_to_operand_aliasing={{0}: (5, {}), {1}: (6, {})} | custom-call | flops 20000000000 | bytes 50331648 | tf_op jit(solution)/shard_map/self_attn/pallas_call | solution.py:143
  102.1 0.0 collective-permute-done.3.refs_4_
  102.1 0.0 collective-permute-done.2.refs_3_
  102.1 21.6 %last.1 = (f32[2,32,768]{2,1,0:T(8,128)}, f32[32,768]{1,0:T(8,128)}) custom-call(s32[16]{0:T(128)} %len_ref.3, f32[32,768]{1,0:T(8,128)} %bitcast.43, f32[32,768]{1,0:T(8,128)} %get-tuple-element.30.x_ref, bf16[2,768]{1,0:T(2,128)(2,1)} %gcross_ref.3, bf16[2,768]{1,0:T(2,128)(2,1)} %gmlp_ref.3, bf16[2,16,768,512]{3,2,1,0:T(8,128)(2,1)} %bitcast.40, ...), custom_call_target="tpu_custom_call" | custom-call | flops 20000000000 | bytes 8388608 | tf_op jit(solution)/shard_map/last/pallas_call | solution.py:544
  123.7 1.6 %fusion.2 = bf16[32,768]{1,0:T(8,128)(2,1)} fusion(f32[32,768]{1,0:T(8,128)} %get-tuple-element.34, f32[2,32,768]{2,1,0:T(8,128)} %get-tuple-element.33), kind=kLoop, calls=%fused_computation.3 | loop fusion | flops 98304 | bytes 344064 | tf_op jit(solution)/shard_map/convert_element_type | solution.py:625
Async XLA Ops:
  26.8 21.1 %collective-permute-start.1 = (bf16[192,2048]{1,0:T(8,128)(2,1)}, bf16[192,2048]{1,0:T(8,128)(2,1)}, u32[]{:S(2)}, u32[]{:S(2)}) collective-permute-start(bf16[192,2048]{1,0:T(8,128)(2,1)} %get-tuple-element.25), channel_id=1, source_target_pairs={{0,2},{1,3},{2,0},{3,1},{4,6},{5,7},{6,4},{7,5}} | collective-permute-start | bytes 2359304 | tf_op jit(solution)/shard_map/ppermute | solution.py:597
  27.3 20.6 %collective-permute-start = (bf16[2,192,1152]{2,1,0:T(8,128)(2,1)}, bf16[2,192,1152]{2,1,0:T(8,128)(2,1)}, u32[]{:S(2)}, u32[]{:S(2)}) collective-permute-start(bf16[2,192,1152]{2,1,0:T(8,128)(2,1)} %get-tuple-element.24.refs_3_), channel_id=1, source_target_pairs={{0,4},{4,0},{1,5},{5,1},{2,6},{6,2},{3,7},{7,3}} | collective-permute-start | bytes 2654216 | tf_op jit(solution)/shard_map/ppermute | solution.py:596
  81.1 21.0 %collective-permute-start.3 = (bf16[192,2048]{1,0:T(8,128)(2,1)}, bf16[192,2048]{1,0:T(8,128)(2,1)}, u32[]{:S(2)}, u32[]{:S(2)}) collective-permute-start(bf16[192,2048]{1,0:T(8,128)(2,1)} %get-tuple-element.32), channel_id=1, source_target_pairs={{0,2},{1,3},{2,0},{3,1},{4,6},{5,7},{6,4},{7,5}} | collective-permute-start | bytes 2359304 | tf_op jit(solution)/shard_map/ppermute | solution.py:597
  81.8 20.3 %collective-permute-start.2 = (bf16[2,192,1152]{2,1,0:T(8,128)(2,1)}, bf16[2,192,1152]{2,1,0:T(8,128)(2,1)}, u32[]{:S(2)}, u32[]{:S(2)}) collective-permute-start(bf16[2,192,1152]{2,1,0:T(8,128)(2,1)} %get-tuple-element.31.refs_2_), channel_id=1, source_target_pairs={{0,4},{4,0},{1,5},{5,1},{2,6},{6,2},{3,7},{7,3}} | collective-permute-start | bytes 2654216 | tf_op jit(solution)/shard_map/ppermute | solution.py:596

commit v6 on v5

--- a/solution.py
+++ b/solution.py
@@ -107,8 +107,8 @@
             here = (lane_row == lane) | (lane_row == lane + 1)
             for n, _, _, buf in sides:
                 ins = dot32(kvt[n], sel)
-                old = buf[b, :, pl.ds(off, wide)].astype(F32)
-                buf[b, :, pl.ds(off, wide)] = jnp.where(here, ins, old).astype(BF16)
+                at = pl.ds(off, wide)
+                buf[b, :, at] = jnp.where(here, ins.astype(BF16), buf[b, :, at])
             for copy in stores(b):
                 copy.start()
         queries = [spread_query(qkv_ref, b, seqs, hmask) for b in seqids]

time: 126 us -> 126 us (level)
  no operation moved by 1% of the time
where the time goes in v6:
time: 126 us; the launch traced here: 125 us
  Pallas kernels  119 us (94%)
  starting transfers between devices  3.95 us (3%)
  other arithmetic  1.63 us (1%)
    pallas_call x3, Pallas kernels, exchange_call(): pl.pallas_call(kernel, out_shape=tuple((t for _, t in outs)), in_specs=sp...  81 us
    pallas_call x2, Pallas kernels, self_attention(): pl.pallas_call(functools.partial(self_kernel, layer, seqs, outs is not No...  38.1 us
    ppermute x2, starting transfers between devices, local_step(): ypack = lax.ppermute(pack, 'col', flip)  2.77 us
  transfers between devices with their start and end apart: 4, of which 0 were waited for; matrix products, arithmetic and copies ran while one was open for 0% of the time, Pallas kernels for 30%

profile of v6, /device:TPU:0, one launch (start us, length us, event | category | flops | bytes accessed | tf_op | source)
XLA Modules:
  0.0 125.3 jit_solution(5424771474071227601)
XLA Ops:
  0.6 26.1 %start.1 = (f32[32,768]{1,0:T(8,128)}, f32[2,32,1152]{2,1,0:T(8,128)}, bf16[2,192,1152]{2,1,0:T(8,128)(2,1)}, bf16[192,2048]{1,0:T(8,128)(2,1)}, f32[16,512]{1,0:T(8,128)}) custom-call(bf16[16,768]{1,0:T(8,128)(2,1)} %first_ref.1, bf16[16,768]{1,0:T(8,128)(2,1)} %second_ref.1, bf16[2,768]{1,0:T(2,128)(2,1)} %refs_0_.1, f32[12,32]{1,0:T(8,128)} %bitcast.44, ...), custom_call_target="tpu_custom_call" | custom-call | flops 3000000000 | bytes 8388608 | tf_op jit(solution)/shard_map/start/pallas_call | solution.py:544
  26.8 0.6 collective-permute-start.1
  27.3 1.5 %collective-permute-start = (bf16[2,192,1152]{2,1,0:T(8,128)(2,1)}, bf16[2,192,1152]{2,1,0:T(8,128)(2,1)}, u32[]{:S(2)}, u32[]{:S(2)}) collective-permute-start(bf16[2,192,1152]{2,1,0:T(8,128)(2,1)} %get-tuple-element.24.refs_3_), channel_id=1, source_target_pairs={{0,4},{4,0},{1,5},{5,1},{2,6},{6,2},{3,7},{7,3}} | collective-permute-start | bytes 2654216 | tf_op jit(solution)/shard_map/ppermute | solution.py:596
  28.8 19.0 %self_attn.2 = (bf16[2,16,768,512]{3,2,1,0:T(8,128)(2,1)}, bf16[2,16,768,512]{3,2,1,0:T(8,128)(2,1)}, f32[2,16,768]{2,1,0:T(8,128)}) custom-call(s32[16]{0:T(128)} %pos_ref.3, f32[2,32,1152]{2,1,0:T(8,128)} %get-tuple-element.20.qkv_ref, f32[16,512]{1,0:T(8,128)} %get-tuple-element.21.tab_ref, bf16[2,16,768,512]{3,2,1,0:T(8,128)(2,1)} %bitcast.32, ...), custom_call_target="tpu_custom_call" | custom-call | flops 20000000000 | bytes 50331648 | tf_op jit(solution)/shard_map/self_attn/pallas_call | solution.py:143
  47.9 0.0 collective-permute-done.1.refs_5_
  47.9 0.0 collective-permute-done.refs_4_
  47.9 33.2 %layer.1 = (f32[32,768]{1,0:T(8,128)}, f32[2,32,1152]{2,1,0:T(8,128)}, bf16[2,192,1152]{2,1,0:T(8,128)(2,1)}, bf16[192,2048]{1,0:T(8,128)(2,1)}) custom-call(s32[16]{0:T(128)} %len_ref.3, f32[32,768]{1,0:T(8,128)} %bitcast.45, f32[32,768]{1,0:T(8,128)} %get-tuple-element.23.x_ref, bf16[2,768]{1,0:T(2,128)(2,1)} %gcross_ref.3, bf16[2,768]{1,0:T(2,128)(2,1)} %gmlp_ref.3, ...), custom_call_target="tpu_custom_call" | custom-call | flops 20000000000 | bytes 8388608 | tf_op jit(solution)/shard_map/layer/pallas_call | solution.py:544
  81.1 0.6 collective-permute-start.3
  81.7 1.3 %collective-permute-start.2 = (bf16[2,192,1152]{2,1,0:T(8,128)(2,1)}, bf16[2,192,1152]{2,1,0:T(8,128)(2,1)}, u32[]{:S(2)}, u32[]{:S(2)}) collective-permute-start(bf16[2,192,1152]{2,1,0:T(8,128)(2,1)} %get-tuple-element.31.refs_2_), channel_id=1, source_target_pairs={{0,4},{4,0},{1,5},{5,1},{2,6},{6,2},{3,7},{7,3}} | collective-permute-start | bytes 2654216 | tf_op jit(solution)/shard_map/ppermute | solution.py:596
  83.0 19.1 %self_attn.3 = (bf16[2,16,768,512]{3,2,1,0:T(8,128)(2,1)}, bf16[2,16,768,512]{3,2,1,0:T(8,128)(2,1)}, f32[2,16,768]{2,1,0:T(8,128)}) custom-call(s32[16]{0:T(128)} %pos_ref.3, f32[2,32,1152]{2,1,0:T(8,128)} %get-tuple-element.26.qkv_ref, f32[16,512]{1,0:T(8,128)} %get-tuple-element.21.tab_ref, ...), custom_call_target="tpu_custom_call", output_to_operand_aliasing={{0}: (5, {}), {1}: (6, {})} | custom-call | flops 20000000000 | bytes 50331648 | tf_op jit(solution)/shard_map/self_attn/pallas_call | solution.py:143
  102.1 0.0 collective-permute-done.3.refs_4_
  102.1 0.0 collective-permute-done.2.refs_3_
  102.1 21.6 %last.1 = (f32[2,32,768]{2,1,0:T(8,128)}, f32[32,768]{1,0:T(8,128)}) custom-call(s32[16]{0:T(128)} %len_ref.3, f32[32,768]{1,0:T(8,128)} %bitcast.43, f32[32,768]{1,0:T(8,128)} %get-tuple-element.30.x_ref, bf16[2,768]{1,0:T(2,128)(2,1)} %gcross_ref.3, bf16[2,768]{1,0:T(2,128)(2,1)} %gmlp_ref.3, bf16[2,16,768,512]{3,2,1,0:T(8,128)(2,1)} %bitcast.40, ...), custom_call_target="tpu_custom_call" | custom-call | flops 20000000000 | bytes 8388608 | tf_op jit(solution)/shard_map/last/pallas_call | solution.py:544
  123.7 1.6 %fusion.2 = bf16[32,768]{1,0:T(8,128)(2,1)} fusion(f32[32,768]{1,0:T(8,128)} %get-tuple-element.34, f32[2,32,768]{2,1,0:T(8,128)} %get-tuple-element.33), kind=kLoop, calls=%fused_computation.3 | loop fusion | flops 98304 | bytes 344064 | tf_op jit(solution)/shard_map/convert_element_type | solution.py:625
Async XLA Ops:
  26.8 21.1 %collective-permute-start.1 = (bf16[192,2048]{1,0:T(8,128)(2,1)}, bf16[192,2048]{1,0:T(8,128)(2,1)}, u32[]{:S(2)}, u32[]{:S(2)}) collective-permute-start(bf16[192,2048]{1,0:T(8,128)(2,1)} %get-tuple-element.25), channel_id=1, source_target_pairs={{0,2},{1,3},{2,0},{3,1},{4,6},{5,7},{6,4},{7,5}} | collective-permute-start | bytes 2359304 | tf_op jit(solution)/shard_map/ppermute | solution.py:597
  27.3 20.5 %collective-permute-start = (bf16[2,192,1152]{2,1,0:T(8,128)(2,1)}, bf16[2,192,1152]{2,1,0:T(8,128)(2,1)}, u32[]{:S(2)}, u32[]{:S(2)}) collective-permute-start(bf16[2,192,1152]{2,1,0:T(8,128)(2,1)} %get-tuple-element.24.refs_3_), channel_id=1, source_target_pairs={{0,4},{4,0},{1,5},{5,1},{2,6},{6,2},{3,7},{7,3}} | collective-permute-start | bytes 2654216 | tf_op jit(solution)/shard_map/ppermute | solution.py:596
  81.1 21.0 %collective-permute-start.3 = (bf16[192,2048]{1,0:T(8,128)(2,1)}, bf16[192,2048]{1,0:T(8,128)(2,1)}, u32[]{:S(2)}, u32[]{:S(2)}) collective-permute-start(bf16[192,2048]{1,0:T(8,128)(2,1)} %get-tuple-element.32), channel_id=1, source_target_pairs={{0,2},{1,3},{2,0},{3,1},{4,6},{5,7},{6,4},{7,5}} | collective-permute-start | bytes 2359304 | tf_op jit(solution)/shard_map/ppermute | solution.py:597
  81.7 20.4 %collective-permute-start.2 = (bf16[2,192,1152]{2,1,0:T(8,128)(2,1)}, bf16[2,192,1152]{2,1,0:T(8,128)(2,1)}, u32[]{:S(2)}, u32[]{:S(2)}) collective-permute-start(bf16[2,192,1152]{2,1,0:T(8,128)(2,1)} %get-tuple-element.31.refs_2_), channel_id=1, source_target_pairs={{0,4},{4,0},{1,5},{5,1},{2,6},{6,2},{3,7},{7,3}} | collective-permute-start | bytes 2654216 | tf_op jit(solution)/shard_map/ppermute | solution.py:596
